TPU v7x, 32 devices: a whole 2x2x4 slice. The times are simulated.
32 devices in a mesh: agent: 2 (over x), row: 4 (over z), col: 4 (over y, core).
Axes of the slice: x: 2, y: 2, z: 4, core: 2. Of those that a mesh axis runs over, the one named last changes fastest.
Arguments:
- probe_field: float32 [2, 256, 256], replicated, may hold values from -4.2 to 4.2
- offsets: int32 [2, 16, 8], P(None, ('agent', 'row'), 'col'), may hold values from -32 to 32
- amplitudes: float32 [16, 8, 256, 256], P(('agent', 'row'), 'col'), may hold values from 0.2 to 2
- data_state: float32 [2, 1024, 512], P(None, ('agent', 'row'), 'col'), may hold values from -4.2 to 4.2
- prior_state: float32 [2, 1024, 512], P(None, ('agent', 'row', 'col')), may hold values from -4.2 to 4.2
- first_weights: bfloat16 [3, 32, 6], replicated, may hold values from -2 to 2
- middle_weights: bfloat16 [4, 3, 32, 96], replicated, may hold values from -0.5 to 0.5
- last_weights: bfloat16 [3, 2, 96], replicated, may hold values from -0.375 to 0.375
Outputs:
- data_next: float32 [2, 1024, 512], P(None, ('agent', 'row'), 'col')
- prior_next: float32 [2, 1024, 512], P(None, ('agent', 'row', 'col'))
All inputs are finite; a program needn't handle non-finite values.
Results may differ from a plain program's by a relative error of at most 0.0073.
Values may be sent and summed in bfloat16 or wider, within the bound.
No kernel may reach another device: no remote copies, remote signals or barrier semaphores. Data moves between devices by JAX's collectives and lax.ppermute only.
A program may use at most 64 MiB of HBM per device.

v0:
```python
import math

import jax
import jax.numpy as jnp
from jax import lax
from jax.sharding import PartitionSpec as P

PROBE = 256
STEP = 64
JITTER = 32
LAYERS = 6
HALO = 128


MAGNITUDE_FLOOR = 0.5
DATA_STEP = 0.125
DATA_WEIGHT = 0.6
RELAXATION = 0.5


def extended_2(block, sides, width):
    for axis, dim in sides:
        count = lax.axis_size(axis)
        forward = [(i, i + 1) for i in range(count - 1)]
        backward = [(target, source) for source, target in forward]
        low = lax.ppermute(
            lax.slice_in_dim(block, block.shape[dim] - width, None, axis=dim), axis, forward
        )
        high = lax.ppermute(lax.slice_in_dim(block, 0, width, axis=dim), axis, backward)
        block = jnp.concatenate([low, block, high], axis=dim)
    return block


def as_index(value):
    return jnp.asarray(value).astype(jnp.int32)


def dft_tables():
    numbers = jnp.arange(PROBE, dtype=jnp.int32)
    product = numbers[:, None] * numbers[None, :] % PROBE
    angles = product.astype(jnp.float32) * (2.0 * math.pi / PROBE)
    scaling = 1.0 / math.sqrt(PROBE)
    return (
        (jnp.cos(angles) * scaling).astype(jnp.bfloat16),
        (-jnp.sin(angles) * scaling).astype(jnp.bfloat16),
    )


def right_product(left_real, left_imag, table_real, table_imag):
    joined = jnp.concatenate([left_real, left_imag], axis=-1)
    table = jnp.concatenate(
        [
            jnp.concatenate([table_real, table_imag], axis=1),
            jnp.concatenate([-table_imag, table_real], axis=1),
        ],
        axis=0,
    )
    output = jnp.einsum("bjk,kw->bjw", joined, table, preferred_element_type=jnp.float32)
    midpoint = left_real.shape[-1]
    return (output[..., :midpoint], output[..., midpoint:])


def left_product(table_real, table_imag, right_real, right_imag):
    stacked = jnp.concatenate([table_real, table_imag], axis=0)
    first = jnp.einsum("jk,bkw->bjw", stacked, right_real, preferred_element_type=jnp.float32)
    second = jnp.einsum("jk,bkw->bjw", stacked, right_imag, preferred_element_type=jnp.float32)
    midpoint = table_real.shape[0]
    return (first[:, :midpoint] - second[:, midpoint:], first[:, midpoint:] + second[:, :midpoint])


def position_terms(patches, measured, probe_field, table_real, table_imag):
    probe_real = probe_field[0]
    probe_imag = probe_field[1]
    object_real = patches[:, 0]
    object_imag = patches[:, 1]
    exit_real = (probe_real * object_real - probe_imag * object_imag).astype(jnp.bfloat16)
    exit_imag = (probe_real * object_imag + probe_imag * object_real).astype(jnp.bfloat16)
    half_real, half_imag = right_product(exit_real, exit_imag, table_real, table_imag)
    wave_real, wave_imag = left_product(
        table_real, table_imag, half_real.astype(jnp.bfloat16), half_imag.astype(jnp.bfloat16)
    )
    magnitude = jnp.sqrt(wave_real * wave_real + wave_imag * wave_imag)
    retained = 1.0 - measured / jnp.maximum(magnitude, MAGNITUDE_FLOOR)
    resid_real = (wave_real * retained).astype(jnp.bfloat16)
    resid_imag = (wave_imag * retained).astype(jnp.bfloat16)
    back_real, back_imag = right_product(resid_real, resid_imag, table_real, -table_imag)
    field_real, field_imag = left_product(
        table_real, -table_imag, back_real.astype(jnp.bfloat16), back_imag.astype(jnp.bfloat16)
    )
    contrib_real = probe_real * field_real + probe_imag * field_imag
    contrib_imag = probe_real * field_imag - probe_imag * field_real
    return jnp.stack([contrib_real, contrib_imag], axis=1)


def fold_margins(array, axis_dim, extent):
    centre = lax.slice_in_dim(array, 2 * HALO, 2 * HALO + extent, axis=axis_dim)
    lower = lax.slice_in_dim(array, 0, HALO, axis=axis_dim)
    upper = lax.slice_in_dim(array, extent + 3 * HALO, extent + 4 * HALO, axis=axis_dim)
    lower_pad = [(0, 0)] * array.ndim
    lower_pad[axis_dim] = (0, extent - HALO)
    upper_pad = [(0, 0)] * array.ndim
    upper_pad[axis_dim] = (extent - HALO, 0)
    return centre + lower + upper


def convolve(current, weight):
    row_count = current.shape[1] - 2
    col_count = current.shape[2]
    widened = jnp.pad(current, ((0, 0), (0, 0), (1, 1)))
    summed = None
    for shift_row in range(3):
        stacked = jnp.concatenate(
            [
                widened[:, shift_row : shift_row + row_count, shift_col : shift_col + col_count]
                for shift_col in range(3)
            ],
            axis=0,
        )
        contribution = jnp.einsum(
            "ok,krw->orw", weight[shift_row], stacked, preferred_element_type=jnp.float32
        )
        summed = contribution if summed is None else summed + contribution
    return summed


def denoise_rows(current, first_row, height, weights):
    output = None
    for depth in range(LAYERS):
        output = convolve(current, weights[depth])
        first_row = first_row + 1
        if depth < LAYERS - 1:
            row_ids = first_row + jnp.arange(output.shape[1], dtype=jnp.int32)
            inside = (row_ids >= 0) & (row_ids < height)
            current = jnp.where(inside[None, :, None], jax.nn.relu(output), 0.0).astype(
                jnp.bfloat16
            )
    return output


def on_device(
    probe_field,
    offsets,
    amplitudes,
    data_state,
    prior_state,
    first_weights,
    middle_weights,
    last_weights,
):
    table_real, table_imag = dft_tables()
    tile_rows = data_state.shape[1]
    tile_cols = data_state.shape[2]
    grid_rows = tile_rows // STEP
    grid_cols = tile_cols // STEP
    anchor_zero = as_index(0)
    extended = extended_2(data_state, ((("agent", "row"), 1), ("col", 2)), HALO)
    ext_rows = extended.shape[1]
    ext_cols = extended.shape[2]
    upper_grid = as_index(
        (jnp.arange(grid_rows, dtype=jnp.int32) * STEP + JITTER)[:, None] + offsets[0]
    )
    left_grid = as_index(
        (jnp.arange(grid_cols, dtype=jnp.int32) * STEP + JITTER)[None, :] + offsets[1]
    )
    upper_edges = upper_grid.reshape(-1)
    left_edges = left_grid.reshape(-1)
    patches = jax.vmap(
        lambda upper_edge, left_edge: lax.dynamic_slice(
            extended, (anchor_zero, as_index(upper_edge), as_index(left_edge)), (2, PROBE, PROBE)
        )
    )(upper_edges, left_edges)
    contributions = position_terms(
        patches, amplitudes.reshape(-1, PROBE, PROBE), probe_field, table_real, table_imag
    )
    contributions = contributions.reshape(grid_rows, grid_cols, 2, PROBE, PROBE)
    probe_ids = jnp.arange(PROBE, dtype=jnp.int32)
    row_ids = jnp.arange(ext_rows, dtype=jnp.int32)
    col_ids = jnp.arange(ext_cols, dtype=jnp.int32)

    def place_row(total, inputs):
        uppers, lefts, terms = inputs
        row_hit = (
            row_ids[None, :, None] == uppers[:, None, None] + probe_ids[None, None, :]
        ).astype(jnp.float32)
        col_hit = (
            lefts[:, None, None] + probe_ids[None, :, None] == col_ids[None, None, :]
        ).astype(jnp.float32)
        spread = jnp.einsum("gkab,gbc->gkac", terms, col_hit, precision=lax.Precision.HIGHEST)
        placed = jnp.einsum("gra,gkac->krc", row_hit, spread, precision=lax.Precision.HIGHEST)
        return (total + placed, None)

    buffer = lax.scan(
        place_row, jnp.zeros(extended.shape, jnp.float32), (upper_grid, left_grid, contributions)
    )[0]
    rims = extended_2(buffer, ((("agent", "row"), 1), ("col", 2)), HALO)
    gradient = fold_margins(fold_margins(rims, 1, tile_rows), 2, tile_cols)
    data_update = data_state - DATA_STEP * gradient
    data_reflect = 2.0 * data_update - data_state
    weights = (
        [first_weights] + [middle_weights[number] for number in range(LAYERS - 2)] + [last_weights]
    )
    inputs = prior_state.astype(jnp.bfloat16)
    strip_rows = prior_state.shape[1]
    widened = extended_2(inputs, ((("agent", "row", "col"), 1),), LAYERS)
    height = strip_rows * lax.axis_size(("agent", "row", "col"))
    first_row = as_index(lax.axis_index(("agent", "row", "col")) * strip_rows - LAYERS)
    noise = denoise_rows(widened, first_row, height, weights)
    prior_update = prior_state - noise
    prior_reflect = 2.0 * prior_update - prior_state
    reflect_tiles = lax.all_to_all(prior_reflect, "col", split_axis=2, concat_axis=1, tiled=True)
    consensus = DATA_WEIGHT * data_reflect + (1.0 - DATA_WEIGHT) * reflect_tiles
    data_next = (1.0 - RELAXATION) * data_state + RELAXATION * (2.0 * consensus - data_reflect)
    consensus_strips = lax.all_to_all(consensus, "col", split_axis=1, concat_axis=2, tiled=True)
    prior_next = (1.0 - RELAXATION) * prior_state + RELAXATION * (
        2.0 * consensus_strips - prior_reflect
    )
    return (data_next, prior_next)


def solution(mesh):
    placed = (
        P(),
        P(None, ("agent", "row"), "col"),
        P(("agent", "row"), "col", None, None),
        P(None, ("agent", "row"), "col"),
        P(None, ("agent", "row", "col"), None),
        P(),
        P(),
        P(),
    )
    return jax.shard_map(
        on_device,
        mesh=mesh,
        in_specs=placed,
        out_specs=(P(None, ("agent", "row"), "col"), P(None, ("agent", "row", "col"), None)),
        check_vma=False,
    )
```

profile of v0, /device:TPU:10, one launch (start us, length us, event | category | flops | bytes accessed | tf_op | source)
XLA Modules:
  0.0 148.6 jit_solution(4708836147452621258)
XLA Ops:
  0.6 3.6 %collective-permute-start = (f32[2,128,128]{2,1,0:T(8,128)}, f32[2,128,128]{2,1,0:T(8,128)}, u32[]{:S(2)}, u32[]{:S(2)}) collective-permute-start(f32[2,128,128]{2,1,0:T(8,128)} %param.13), channel_id=1, source_target_pairs={{0,4},{4,8},{8,12},{12,16},{16,20},{20,24},{24,28},{1,5},{5,9},{9,... | collective-permute-start | bytes 393224 | tf_op jit(solution)/shard_map/ppermute | solution.py:26
  4.3 2.4 %collective-permute-start.1 = (f32[2,128,128]{2,1,0:T(8,128)}, f32[2,128,128]{2,1,0:T(8,128)}, u32[]{:S(2)}, u32[]{:S(2)}) collective-permute-start(f32[2,128,128]{2,1,0:T(8,128)} %param.13), channel_id=1, source_target_pairs={{4,0},{8,4},{12,8},{16,12},{20,16},{24,20},{28,24},{5,1},{9,5},{13... | collective-permute-start | bytes 393224 | tf_op jit(solution)/shard_map/ppermute | solution.py:29
  6.6 1.0 copy.118
  7.7 4.9 %collective-permute-start.9 = (bf16[2,6,512]{2,0,1:T(2,128)(2,1)S(1)}, bf16[2,6,512]{2,0,1:T(2,128)(2,1)S(1)}, u32[]{:S(2)}, u32[]{:S(2)}) collective-permute-start(bf16[2,6,512]{2,0,1:T(2,128)(2,1)S(1)} %get-tuple-element.229), channel_id=1, source_target_pairs={{1,0},{2,1},{3,2},{4,3},{5,4},{6,5},{7,6},{8,7},{9,8},{10,9},{11,1... | collective-permute-start | bytes 36872 | tf_op jit(solution)/shard_map/ppermute | solution.py:29
  12.6 1.9 %collective-permute-start.8 = (bf16[2,6,512]{2,0,1:T(2,128)(2,1)S(1)}, bf16[2,6,512]{2,0,1:T(2,128)(2,1)S(1)}, u32[]{:S(2)}, u32[]{:S(2)}) collective-permute-start(bf16[2,6,512]{2,0,1:T(2,128)(2,1)S(1)} %get-tuple-element.228), channel_id=1, source_target_pairs={{0,1},{1,2},{2,3},{3,4},{4,5},{5,6},{6,7},{7,8},{8,9},{9,10},{10,1... | collective-permute-start | bytes 36872 | tf_op jit(solution)/shard_map/ppermute | solution.py:26
  14.5 1.7 %multiply_convert_fusion.2 = (bf16[256,256]{1,0:T(8,128)(2,1)}, bf16[256,256]{1,0:T(8,128)(2,1)S(1)}) fusion(), kind=kLoop, calls=%fused_computation.245 | loop fusion | flops 1245184 | bytes 262144 | tf_op jit(solution)/shard_map/convert_element_type | solution.py:45
  16.2 1.6 %fusion.204 = bf16[256,256]{1,0:T(8,128)(2,1)} fusion(), kind=kLoop, calls=%fused_computation.265 | loop fusion | flops 1310720 | bytes 131072 | tf_op jit(solution)/shard_map/neg | solution.py:54
  19.5 1.9 %slice_bitcast_fusion.1 = (f32[256,256]{1,0:T(8,128)}, f32[256,256]{1,0:T(8,128)}) fusion(f32[2,256,256]{2,1,0:T(8,128)} %param.10), kind=kLoop, calls=%fused_computation.250 | loop fusion | bytes 1048576 | tf_op jit(solution)/shard_map/mul | solution.py:90
  25.9 1.2 fusion.115
  27.1 4.8 %pad_slice_fusion.3 = (bf16[32,40,512]{2,0,1:T(8,128)(2,1)S(1)}, bf16[32,40,512]{2,0,1:T(8,128)(2,1)S(1)}, bf16[32,40,512]{2,0,1:T(8,128)(2,1)S(1)}, bf16[32,40,...) fusion(bf16[32,42,512]{2,0,1:T(8,128)(2,1)S(1)} %fusion.115), kind=kLoop, calls=%fused_computation.125 | loop fusion | bytes 17104896 | tf_op jit(solution)/shard_map/slice | solution.py:114
  33.3 0.9 fusion.116
  34.2 4.3 %pad_slice_fusion.9 = (bf16[32,38,512]{2,0,1:T(8,128)(2,1)S(1)}, bf16[32,38,512]{2,0,1:T(8,128)(2,1)S(1)}, bf16[32,38,512]{2,0,1:T(8,128)(2,1)S(1)}, bf16[32,38,...) fusion(bf16[32,40,512]{2,0,1:T(8,128)(2,1)S(1)} %fusion.116), kind=kLoop, calls=%fused_computation.133 | loop fusion | bytes 16252928 | tf_op jit(solution)/shard_map/slice | solution.py:114
  39.8 0.9 fusion.119
  40.7 4.2 %pad_slice_fusion.15 = (bf16[32,36,512]{2,0,1:T(8,128)(2,1)S(1)}, bf16[32,36,512]{2,0,1:T(8,128)(2,1)S(1)}, bf16[32,36,512]{2,0,1:T(8,128)(2,1)S(1)}, bf16[32,36...) fusion(bf16[32,38,512]{2,0,1:T(8,128)(2,1)S(1)} %fusion.119), kind=kLoop, calls=%fused_computation.142 | loop fusion | bytes 15400960 | tf_op jit(solution)/shard_map/slice | solution.py:114
  47.0 4.1 %pad_slice_fusion.21 = (bf16[32,34,512]{2,0,1:T(8,128)(2,1)S(1)}, bf16[32,34,512]{2,0,1:T(8,128)(2,1)S(1)}, bf16[32,34,512]{2,0,1:T(8,128)(2,1)S(1)}, bf16[32,34...) fusion(bf16[32,36,512]{2,0,1:T(8,128)(2,1)S(1)} %fusion.122), kind=kLoop, calls=%fused_computation.150 | loop fusion | bytes 14548992 | tf_op jit(solution)/shard_map/slice | solution.py:114
  52.3 0.8 fusion.125
  53.2 0.9 constant_dynamic-update-slice_fusion.2
  54.1 0.9 constant_dynamic-update-slice_fusion
  55.0 1.3 collective-permute-start.3
  56.3 3.1 %collective-permute-start.2 = (f32[2,384,128]{2,1,0:T(8,128)S(1)}, f32[2,384,128]{2,1,0:T(8,128)S(1)}, u32[]{:S(2)}, u32[]{:S(2)}) collective-permute-start(f32[2,384,128]{2,1,0:T(8,128)S(1)} %constant_dynamic-update-slice_fusion), channel_id=1, source_target_pairs={{0,1},{1,2},{2,3},{4,5},{5,6},{6,7},{8,9},{9,10},{10,11},{12,13},{... | collective-permute-start | bytes 1179656 | tf_op jit(solution)/shard_map/ppermute | solution.py:26
  59.4 5.9 %pad_slice_fusion.25 = (bf16[32,32,512]{2,0,1:T(8,128)(2,1)}, bf16[32,32,512]{2,0,1:T(8,128)(2,1)}, bf16[32,32,512]{2,0,1:T(8,128)(2,1)}, bf16[32,32,512]{2,0,1:...) fusion(bf16[32,34,512]{2,0,1:T(8,128)(2,1)S(1)} %fusion.125), kind=kLoop, calls=%fused_computation.154 | loop fusion | bytes 13697024 | tf_op jit(solution)/shard_map/slice | solution.py:114
  65.4 11.8 %while.14 = (s32[]{:T(128)}, f32[2,384,384]{2,1,0:T(8,128)S(1)}, s32[4,3]{1,0:T(4,128)S(1)}, f32[4,2,256,256]{3,2,0,1:T(8,128)}, s32[]{:T(128)}) while((s32[]{:T(128)}, f32[2,384,384]{2,1,0:T(8,128)S(1)}, s32[4,3]{1,0:T(4,128)S(1)}, f32[4,2,256,256]{3,2,0,1:T(8,128)}, s32[]{:T(128)}) %tuple.117), condition=%wide.while_cond, body=%wide.while_body.sunk | while | flops 2 | bytes 1049717 | solution.py:168
  66.1 2.3 %bitcast_dynamic-update-slice_fusion.2 = f32[4,2,256,256]{3,2,0,1:T(8,128)} fusion(f32[4,2,256,256]{3,2,0,1:T(8,128)} %get-tuple-element.310, s32[]{:T(128)S(6)} %copy.126, f32[2,384,384]{2,1,0:T(8,128)S(1)} %get-tuple-element.313, s32[]{:T(128)} %bitcast.217, s32[]{:T(128)} %bitcast.218), kind=kLoop, calls=%fused_computation.2.clone.1 | loop fusion | bytes 1049604 | tf_op jit(solution)/shard_map/vmap()/gather
  69.0 2.3 %bitcast_dynamic-update-slice_fusion.2 = f32[4,2,256,256]{3,2,0,1:T(8,128)} fusion(f32[4,2,256,256]{3,2,0,1:T(8,128)} %get-tuple-element.310, s32[]{:T(128)S(6)} %copy.126, f32[2,384,384]{2,1,0:T(8,128)S(1)} %get-tuple-element.313, s32[]{:T(128)} %bitcast.217, s32[]{:T(128)} %bitcast.218), kind=kLoop, calls=%fused_computation.2.clone.1 | loop fusion | bytes 1049604 | tf_op jit(solution)/shard_map/vmap()/gather
  71.9 2.3 %bitcast_dynamic-update-slice_fusion.2 = f32[4,2,256,256]{3,2,0,1:T(8,128)} fusion(f32[4,2,256,256]{3,2,0,1:T(8,128)} %get-tuple-element.310, s32[]{:T(128)S(6)} %copy.126, f32[2,384,384]{2,1,0:T(8,128)S(1)} %get-tuple-element.313, s32[]{:T(128)} %bitcast.217, s32[]{:T(128)} %bitcast.218), kind=kLoop, calls=%fused_computation.2.clone.1 | loop fusion | bytes 1049604 | tf_op jit(solution)/shard_map/vmap()/gather
  74.9 2.3 %bitcast_dynamic-update-slice_fusion.2 = f32[4,2,256,256]{3,2,0,1:T(8,128)} fusion(f32[4,2,256,256]{3,2,0,1:T(8,128)} %get-tuple-element.310, s32[]{:T(128)S(6)} %copy.126, f32[2,384,384]{2,1,0:T(8,128)S(1)} %get-tuple-element.313, s32[]{:T(128)} %bitcast.217, s32[]{:T(128)} %bitcast.218), kind=kLoop, calls=%fused_computation.2.clone.1 | loop fusion | bytes 1049604 | tf_op jit(solution)/shard_map/vmap()/gather
  77.2 2.0 %fusion.154 = (bf16[4,256,256]{2,1,0:T(8,128)(2,1)S(1)}, bf16[4,256,256]{2,1,0:T(8,128)(2,1)S(1)}) fusion(f32[4,2,256,256]{3,2,0,1:T(8,128)} %get-tuple-element.73, f32[256,256]{1,0:T(8,128)} %get-tuple-element.218, f32[256,256]{1,0:T(8,128)} %get-tuple-element.217), kind=kLoop, calls=%fused_computation.181 | loop fusion | flops 2097152 | bytes 3670016 | tf_op jit(solution)/shard_map/convert_element_type | solution.py:76
  84.1 1.5 pad_maximum_fusion
  85.6 8.4 %while.15 = (s32[]{:T(128)}, f32[2,384,384]{1,2,0:T(8,128)S(1)}, f32[2,2,2,256,256]{4,3,1,2,0:T(8,128)}, s32[2,2]{1,0:T(2,128)S(1)}, s32[2,2]{1,0:T(2,128)S(1)}, /*index=5*/s32[]{:T(128)}, s32[]{:T(128)}) while((s32[]{:T(128)}, f32[2,384,384]{1,2,0:T(8,128)S(1)}, f32[2,2,2,256,256]{4,3,1,2,0:T(8,128)}, ...), condition=%wide.region_1.2_spmd.clone.clone, body=%wide.region_0.1_spmd.clone.clone.sunk | while | flops 3020882944 | bytes 6561943 | solution.py:192
  85.7 2.2 %fusion.285 = f32[2,2,256,384]{2,3,0,1:T(8,128)S(1)} fusion(f32[2,2,2,256,256]{4,3,1,2,0:T(8,128)} %get-tuple-element.333, s32[]{:T(128)S(6)} %copy.132, s32[2,256]{1,0:T(2,128)S(1)} %iota_add_fusion.4), kind=kOutput, calls=%fused_computation.6.clone.1 | convolution fusion | flops 1208156160 | bytes 2623492 | tf_op jit(solution)/shard_map/while/body/eval_jaxpr/gkab,gbc->gkac/dot_general | solution.py:188
  87.9 1.9 %fusion.286 = f32[2,384,384]{1,2,0:T(8,128)S(1)} fusion(f32[2,2,256,384]{2,3,0,1:T(8,128)S(1)} %fusion.285, f32[2,384,384]{1,2,0:T(8,128)S(1)} %get-tuple-element.325, pred[]{:T(512)S(6)} %compare.12, s32[2,256]{1,0:T(2,128)S(1)} %iota_add_fusion.5), kind=kOutput, calls=%fused_computation.5.clone.1 | convolution fusion | flops 1812725760 | bytes 3934209 | tf_op jit(solution)/shard_map/while/body/eval_jaxpr/gra,gkac->krc/dot_general | solution.py:189
  89.9 2.2 %fusion.285 = f32[2,2,256,384]{2,3,0,1:T(8,128)S(1)} fusion(f32[2,2,2,256,256]{4,3,1,2,0:T(8,128)} %get-tuple-element.333, s32[]{:T(128)S(6)} %copy.132, s32[2,256]{1,0:T(2,128)S(1)} %iota_add_fusion.4), kind=kOutput, calls=%fused_computation.6.clone.1 | convolution fusion | flops 1208156160 | bytes 2623492 | tf_op jit(solution)/shard_map/while/body/eval_jaxpr/gkab,gbc->gkac/dot_general | solution.py:188
  92.2 1.9 %fusion.286 = f32[2,384,384]{1,2,0:T(8,128)S(1)} fusion(f32[2,2,256,384]{2,3,0,1:T(8,128)S(1)} %fusion.285, f32[2,384,384]{1,2,0:T(8,128)S(1)} %get-tuple-element.325, pred[]{:T(512)S(6)} %compare.12, s32[2,256]{1,0:T(2,128)S(1)} %iota_add_fusion.5), kind=kOutput, calls=%fused_computation.5.clone.1 | convolution fusion | flops 1812725760 | bytes 3934209 | tf_op jit(solution)/shard_map/while/body/eval_jaxpr/gra,gkac->krc/dot_general | solution.py:189
  94.5 3.2 %collective-permute-start.5 = (f32[2,128,384]{2,1,0:T(8,128)S(1)}, f32[2,128,384]{2,1,0:T(8,128)S(1)}, u32[]{:S(2)}, u32[]{:S(2)}) collective-permute-start(f32[2,128,384]{2,1,0:T(8,128)S(1)} %get-tuple-element.198), channel_id=1, source_target_pairs={{4,0},{8,4},{12,8},{16,12},{20,16},{24,20},{28,24},{5,1},{9,5},{13... | collective-permute-start | bytes 1179656 | tf_op jit(solution)/shard_map/ppermute | solution.py:29
  97.7 2.6 %collective-permute-start.4 = (f32[2,128,384]{2,1,0:T(8,128)S(1)}, f32[2,128,384]{2,1,0:T(8,128)S(1)}, u32[]{:S(2)}, u32[]{:S(2)}) collective-permute-start(f32[2,128,384]{2,1,0:T(8,128)S(1)} %get-tuple-element.197), channel_id=1, source_target_pairs={{0,4},{4,8},{8,12},{12,16},{16,20},{20,24},{24,28},{1,5},{5,9},{9,... | collective-permute-start | bytes 1179656 | tf_op jit(solution)/shard_map/ppermute | solution.py:26
  100.4 2.5 %fusion.89 = f32[32,512,2]{1,2,0:T(2,128)S(1)} fusion(bf16[32,32,512]{2,0,1:T(8,128)(2,1)} %get-tuple-element.209, bf16[32,32,512]{2,0,1:T(8,128)(2,1)} %get-tuple-element.215, bf16[32,32,512]{2,0,1:T(8,128)(2,1)} %get-tuple-element.216, bf16[3,2,96]{2,1,0:T(2,128)(2,1)S(1)} %copy-done.17), kind=kOutput, calls=%fused_computation.94 | convolution fusion | flops 15728640 | bytes 3277312 | tf_op jit(solution)/shard_map/ok,krw->orw/dot_general | solution.py:119
  103.7 3.7 %collective-permute-done.5 = f32[2,128,384]{2,1,0:T(8,128)S(1)} collective-permute-done((f32[2,128,384]{2,1,0:T(8,128)S(1)}, f32[2,128,384]{2,1,0:T(8,128)S(1)}, u32[]{:S(2)}, u32[]{:S(2)}) %collective-permute-start.5) | collective-permute-done | bytes 393248 | tf_op jit(solution)/shard_map/ppermute | solution.py:29
  107.4 8.8 %collective-permute-done.4 = f32[2,128,384]{2,1,0:T(8,128)S(1)} collective-permute-done((f32[2,128,384]{2,1,0:T(8,128)S(1)}, f32[2,128,384]{2,1,0:T(8,128)S(1)}, u32[]{:S(2)}, u32[]{:S(2)}) %collective-permute-start.4) | collective-permute-done | bytes 393248 | tf_op jit(solution)/shard_map/ppermute | solution.py:26
  116.2 1.2 pad_maximum_fusion.14
  117.4 1.3 collective-permute-start.7
  118.7 4.0 %collective-permute-start.6 = (f32[2,640,128]{2,1,0:T(8,128)}, f32[2,640,128]{2,1,0:T(8,128)}, u32[]{:S(2)}, u32[]{:S(2)}) collective-permute-start(f32[2,640,128]{2,1,0:T(8,128)} %get-tuple-element.168), channel_id=1, source_target_pairs={{0,1},{1,2},{2,3},{4,5},{5,6},{6,7},{8,9},{9,10},{10,11},{12,13},{... | collective-permute-start | bytes 1966088 | tf_op jit(solution)/shard_map/ppermute | solution.py:26
  124.0 8.9 %all_to_all.8 = f32[4,1,8192]{2,1,0:T(1,128)S(1)} all-to-all(f32[4,1,8192]{2,1,0:T(1,128)S(1)} %reshape.266), channel_id=1, replica_groups=mesh['agent'=2,'row'=4,'col'=4] {'col'}, dimensions={0} | all-to-all | bytes 262144 | tf_op jit(solution)/shard_map/all_to_all | solution.py:210
  133.4 1.0 reduce
  135.3 1.4 pad_maximum_fusion.11
  136.7 1.2 copy_add_fusion
  137.9 0.9 bitcast_add_fusion
  138.9 3.9 %all-to-all-start.1 = ((f32[2,128,128]{2,0,1:T(2,128)}), f32[2,128,128]{2,0,1:T(2,128)S(1)}, u32[]{:S(2)}, u32[]{:S(2)}) async-start(f32[2,128,128]{2,0,1:T(2,128)} %get-tuple-element.153), calls=%async_computation.1 | async-start | bytes 262144 | tf_op jit(solution)/shard_map/all_to_all | solution.py:213
  143.7 3.8 %all-to-all-done.1 = f32[2,128,128]{2,0,1:T(2,128)S(1)} async-done(((f32[2,128,128]{2,0,1:T(2,128)}), f32[2,128,128]{2,0,1:T(2,128)S(1)}, u32[]{:S(2)}, u32[]{:S(2)}) %all-to-all-start.1) | async-done | bytes 131104 | tf_op jit(solution)/shard_map/all_to_all | solution.py:213
  (126 shorter events, 25.7 us)
Async XLA Ops:
  0.6 22.7 %copy-start.6 = (f32[2,2,256,256]{3,2,1,0:T(8,128)S(1)}, f32[2,2,256,256]{3,2,1,0:T(8,128)}, u32[]{:S(2)}) copy-start(f32[2,2,256,256]{3,2,1,0:T(8,128)} %param.12) | copy-start | bytes 3145732
  0.6 52.5 %collective-permute-start = (f32[2,128,128]{2,1,0:T(8,128)}, f32[2,128,128]{2,1,0:T(8,128)}, u32[]{:S(2)}, u32[]{:S(2)}) collective-permute-start(f32[2,128,128]{2,1,0:T(8,128)} %param.13), channel_id=1, source_target_pairs={{0,4},{4,8},{8,12},{12,16},{16,20},{20,24},{24,28},{1,5},{5,9},{9,... | collective-permute-start | bytes 393224 | tf_op jit(solution)/shard_map/ppermute | solution.py:26
  4.3 49.8 %collective-permute-start.1 = (f32[2,128,128]{2,1,0:T(8,128)}, f32[2,128,128]{2,1,0:T(8,128)}, u32[]{:S(2)}, u32[]{:S(2)}) collective-permute-start(f32[2,128,128]{2,1,0:T(8,128)} %param.13), channel_id=1, source_target_pairs={{4,0},{8,4},{12,8},{16,12},{20,16},{24,20},{28,24},{5,1},{9,5},{13... | collective-permute-start | bytes 393224 | tf_op jit(solution)/shard_map/ppermute | solution.py:29
  7.7 16.1 %collective-permute-start.9 = (bf16[2,6,512]{2,0,1:T(2,128)(2,1)S(1)}, bf16[2,6,512]{2,0,1:T(2,128)(2,1)S(1)}, u32[]{:S(2)}, u32[]{:S(2)}) collective-permute-start(bf16[2,6,512]{2,0,1:T(2,128)(2,1)S(1)} %get-tuple-element.229), channel_id=1, source_target_pairs={{1,0},{2,1},{3,2},{4,3},{5,4},{6,5},{7,6},{8,7},{9,8},{10,9},{11,1... | collective-permute-start | bytes 36872 | tf_op jit(solution)/shard_map/ppermute | solution.py:29
  12.6 11.2 %collective-permute-start.8 = (bf16[2,6,512]{2,0,1:T(2,128)(2,1)S(1)}, bf16[2,6,512]{2,0,1:T(2,128)(2,1)S(1)}, u32[]{:S(2)}, u32[]{:S(2)}) collective-permute-start(bf16[2,6,512]{2,0,1:T(2,128)(2,1)S(1)} %get-tuple-element.228), channel_id=1, source_target_pairs={{0,1},{1,2},{2,3},{3,4},{4,5},{5,6},{6,7},{7,8},{8,9},{9,10},{10,1... | collective-permute-start | bytes 36872 | tf_op jit(solution)/shard_map/ppermute | solution.py:26
  19.5 5.1 %copy-start.15 = (bf16[3,32,6]{1,2,0:T(8,128)(2,1)S(1)}, bf16[3,32,6]{1,2,0:T(8,128)(2,1)}, u32[]{:S(2)}) copy-start(bf16[3,32,6]{1,2,0:T(8,128)(2,1)} %param.15) | copy-start | bytes 3460
  27.1 4.9 %copy-start.16 = (bf16[4,3,32,96]{3,2,1,0:T(8,128)(2,1)S(1)}, bf16[4,3,32,96]{3,2,1,0:T(8,128)(2,1)}, u32[]{:S(2)}) copy-start(bf16[4,3,32,96]{3,2,1,0:T(8,128)(2,1)} %param.16) | copy-start | bytes 221188
  32.6 0.7 copy-start.20
  39.2 0.6 copy-start.19
  45.5 0.6 copy-start.18
  52.3 1.8 %copy-start.4 = (f32[2,128,128]{2,1,0:T(8,128)S(1)}, f32[2,128,128]{2,1,0:T(8,128)}, u32[]{:S(2)}) copy-start(f32[2,128,128]{2,1,0:T(8,128)} %param.13) | copy-start | bytes 393220
  55.0 10.3 %collective-permute-start.3 = (f32[2,384,128]{2,1,0:T(8,128)S(1)}, f32[2,384,128]{2,1,0:T(8,128)S(1)}, u32[]{:S(2)}, u32[]{:S(2)}) collective-permute-start(f32[2,384,128]{2,1,0:T(8,128)S(1)} %constant_dynamic-update-slice_fusion), channel_id=1, source_target_pairs={{1,0},{2,1},{3,2},{5,4},{6,5},{7,6},{9,8},{10,9},{11,10},{13,12},{... | collective-permute-start | bytes 1179656 | tf_op jit(solution)/shard_map/ppermute | solution.py:29
  56.3 9.0 %collective-permute-start.2 = (f32[2,384,128]{2,1,0:T(8,128)S(1)}, f32[2,384,128]{2,1,0:T(8,128)S(1)}, u32[]{:S(2)}, u32[]{:S(2)}) collective-permute-start(f32[2,384,128]{2,1,0:T(8,128)S(1)} %constant_dynamic-update-slice_fusion), channel_id=1, source_target_pairs={{0,1},{1,2},{2,3},{4,5},{5,6},{6,7},{8,9},{9,10},{10,11},{12,13},{... | collective-permute-start | bytes 1179656 | tf_op jit(solution)/shard_map/ppermute | solution.py:26
  77.2 2.0 %copy-start.2 = (bf16[256,256]{1,0:T(8,128)(2,1)S(1)}, bf16[256,256]{1,0:T(8,128)(2,1)}, u32[]{:S(2)}) copy-start(bf16[256,256]{1,0:T(8,128)(2,1)} %fusion.204) | copy-start | bytes 393220
  77.2 2.0 %copy-start.3 = (bf16[256,256]{1,0:T(8,128)(2,1)S(1)}, bf16[256,256]{1,0:T(8,128)(2,1)}, u32[]{:S(2)}) copy-start(bf16[256,256]{1,0:T(8,128)(2,1)} %get-tuple-element.236) | copy-start | bytes 393220
  82.7 1.0 copy-start
  82.8 1.0 copy-start.1
  94.0 6.3 %copy-start.17 = (bf16[3,2,96]{2,1,0:T(2,128)(2,1)S(1)}, bf16[3,2,96]{2,1,0:T(2,128)(2,1)}, u32[]{:S(2)}) copy-start(bf16[3,2,96]{2,1,0:T(2,128)(2,1)} %param.17) | copy-start | bytes 3460
  94.5 12.9 %collective-permute-start.5 = (f32[2,128,384]{2,1,0:T(8,128)S(1)}, f32[2,128,384]{2,1,0:T(8,128)S(1)}, u32[]{:S(2)}, u32[]{:S(2)}) collective-permute-start(f32[2,128,384]{2,1,0:T(8,128)S(1)} %get-tuple-element.198), channel_id=1, source_target_pairs={{4,0},{8,4},{12,8},{16,12},{20,16},{24,20},{28,24},{5,1},{9,5},{13... | collective-permute-start | bytes 1179656 | tf_op jit(solution)/shard_map/ppermute | solution.py:29
  97.7 18.5 %collective-permute-start.4 = (f32[2,128,384]{2,1,0:T(8,128)S(1)}, f32[2,128,384]{2,1,0:T(8,128)S(1)}, u32[]{:S(2)}, u32[]{:S(2)}) collective-permute-start(f32[2,128,384]{2,1,0:T(8,128)S(1)} %get-tuple-element.197), channel_id=1, source_target_pairs={{0,4},{4,8},{8,12},{12,16},{16,20},{20,24},{24,28},{1,5},{5,9},{9,... | collective-permute-start | bytes 1179656 | tf_op jit(solution)/shard_map/ppermute | solution.py:26
  100.4 2.6 %copy-start.10 = (bf16[32,32,512]{2,0,1:T(8,128)(2,1)S(1)}, bf16[32,32,512]{2,0,1:T(8,128)(2,1)}, u32[]{:S(2)}) copy-start(bf16[32,32,512]{2,0,1:T(8,128)(2,1)} %get-tuple-element.210) | copy-start | bytes 3145732
  100.4 2.6 %copy-start.11 = (bf16[32,32,512]{2,0,1:T(8,128)(2,1)S(1)}, bf16[32,32,512]{2,0,1:T(8,128)(2,1)}, u32[]{:S(2)}) copy-start(bf16[32,32,512]{2,0,1:T(8,128)(2,1)} %get-tuple-element.211) | copy-start | bytes 3145732
  100.4 2.8 %copy-start.12 = (bf16[32,32,512]{2,0,1:T(8,128)(2,1)S(1)}, bf16[32,32,512]{2,0,1:T(8,128)(2,1)}, u32[]{:S(2)}) copy-start(bf16[32,32,512]{2,0,1:T(8,128)(2,1)} %get-tuple-element.214) | copy-start | bytes 3145732
  103.7 19.0 %copy-start.7 = (bf16[32,32,512]{2,0,1:T(8,128)(2,1)S(1)}, bf16[32,32,512]{2,0,1:T(8,128)(2,1)}, u32[]{:S(2)}) copy-start(bf16[32,32,512]{2,0,1:T(8,128)(2,1)} %get-tuple-element.208) | copy-start | bytes 3145732
  103.7 19.0 %copy-start.8 = (bf16[32,32,512]{2,0,1:T(8,128)(2,1)S(1)}, bf16[32,32,512]{2,0,1:T(8,128)(2,1)}, u32[]{:S(2)}) copy-start(bf16[32,32,512]{2,0,1:T(8,128)(2,1)} %get-tuple-element.212) | copy-start | bytes 3145732
  103.7 19.0 %copy-start.9 = (bf16[32,32,512]{2,0,1:T(8,128)(2,1)S(1)}, bf16[32,32,512]{2,0,1:T(8,128)(2,1)}, u32[]{:S(2)}) copy-start(bf16[32,32,512]{2,0,1:T(8,128)(2,1)} %get-tuple-element.213) | copy-start | bytes 3145732
  103.7 19.0 %copy-start.13 = (f32[2,32,512]{2,1,0:T(8,128)S(1)}, f32[2,32,512]{2,1,0:T(8,128)}, u32[]{:S(2)}) copy-start(f32[2,32,512]{2,1,0:T(8,128)} %param.14) | copy-start | bytes 393220
  117.4 17.9 %collective-permute-start.7 = (f32[2,640,128]{2,1,0:T(8,128)}, f32[2,640,128]{2,1,0:T(8,128)}, u32[]{:S(2)}, u32[]{:S(2)}) collective-permute-start(f32[2,640,128]{2,1,0:T(8,128)} %get-tuple-element.169), channel_id=1, source_target_pairs={{1,0},{2,1},{3,2},{5,4},{6,5},{7,6},{9,8},{10,9},{11,10},{13,12},{... | collective-permute-start | bytes 1966088 | tf_op jit(solution)/shard_map/ppermute | solution.py:29
  118.7 16.6 %collective-permute-start.6 = (f32[2,640,128]{2,1,0:T(8,128)}, f32[2,640,128]{2,1,0:T(8,128)}, u32[]{:S(2)}, u32[]{:S(2)}) collective-permute-start(f32[2,640,128]{2,1,0:T(8,128)} %get-tuple-element.168), channel_id=1, source_target_pairs={{0,1},{1,2},{2,3},{4,5},{5,6},{6,7},{8,9},{9,10},{10,11},{12,13},{... | collective-permute-start | bytes 1966088 | tf_op jit(solution)/shard_map/ppermute | solution.py:26
  136.7 1.2 copy-start.5
  136.7 11.0 %copy-start.14 = (f32[2,32,512]{2,1,0:T(8,128)S(1)}, f32[2,32,512]{2,1,0:T(8,128)}, u32[]{:S(2)}) copy-start(f32[2,32,512]{2,1,0:T(8,128)} %param.14) | copy-start | bytes 393220
  138.9 8.6 %all-to-all-start.1 = ((f32[2,128,128]{2,0,1:T(2,128)}), f32[2,128,128]{2,0,1:T(2,128)S(1)}, u32[]{:S(2)}, u32[]{:S(2)}) async-start(f32[2,128,128]{2,0,1:T(2,128)} %get-tuple-element.153), calls=%async_computation.1 | async-start | bytes 262144 | tf_op jit(solution)/shard_map/all_to_all | solution.py:213
where the time goes:
time: 149 us
  local copies, waits for them, and re-layouts  46.9 us (31%)
  starting transfers between devices  32.1 us (22%)
  matrix products  25.8 us (17%)
  other arithmetic  17.1 us (11%)
  waiting for transfers between devices  16.3 us (11%)
  blocking collectives  8.87 us (6%)
    slice x6, local copies, waits for them, and re-layouts, convolve(): widened[:, shift_row:shift_row + row_count, shift_col:shift_col + col_count]  24.1 us
    ppermute x5, starting transfers between devices, extended_2(): lax.ppermute(lax.slice_in_dim(block, block.shape[dim] - width, None, axis...  15.2 us
    dot_general x18, matrix products, convolve(): jnp.einsum('ok,krw->orw', weight[shift_row], stacked, preferred_element_t...  14.4 us
    ppermute x5, starting transfers between devices, extended_2(): lax.ppermute(lax.slice_in_dim(block, 0, width, axis=dim), axis, backward)  13 us
    gather x12, local copies, waits for them, and re-layouts  11.7 us
    all_to_all x1, blocking collectives, on_device(): lax.all_to_all(prior_reflect, 'col', split_axis=2, concat_axis=1, tiled=T...  8.87 us
    ppermute x5, waiting for transfers between devices, extended_2(): lax.ppermute(lax.slice_in_dim(block, block.shape[dim] - width, None, axis...  8.85 us
    unnamed x51, local copies, waits for them, and re-layouts  5.61 us
  transfers between devices with their start and end apart: 11, of which 3 were waited for; matrix products, arithmetic and copies ran while one was open for 36% of the time, Pallas kernels for 0%

commit v1 on v0

v1 whole, which is shorter than its diff:
```python
import functools
import math

import jax
import jax.numpy as jnp
import numpy as np
from jax import lax
from jax.experimental import pallas as pl
from jax.experimental.pallas import tpu as pltpu
from jax.sharding import PartitionSpec as P

PROBE = 256
STEP = 64
JITTER = 32
LAYERS = 6
HALO = 128
EDGE = 8
BAND = 4
LAST_BAND = 16

MAGNITUDE_FLOOR = 0.5
DATA_STEP = 0.125
DATA_WEIGHT = 0.6
RELAXATION = 0.5

ROWS = ("agent", "row")
STRIPS = ("agent", "row", "col")

VMEM = pl.BlockSpec(memory_space=pltpu.VMEM)
SMEM = pl.BlockSpec(memory_space=pltpu.SMEM)
BF16 = jnp.bfloat16
F32 = jnp.float32


def params(mib=48):
    return pltpu.CompilerParams(vmem_limit_bytes=mib * 1024 * 1024)


def dft_blocks():
    numbers = np.arange(PROBE)
    angles = (numbers[:, None] * numbers[None, :] % PROBE) * (2.0 * math.pi / PROBE)
    real = np.cos(angles) / math.sqrt(PROBE)
    imag = -np.sin(angles) / math.sqrt(PROBE)
    forward = np.block([[real, imag], [-imag, real]])
    return jnp.asarray(forward, BF16), jnp.asarray(forward.T.copy(), BF16)


def ring(value, axes, shift):
    count = lax.axis_size(axes)
    return lax.ppermute(value, axes, [(i, (i + shift) % count) for i in range(count)])


def band_kernel(strip, first_ref, middle_ref, last_ref, t1_ref, tm_ref, t6_ref, lane_ref, few_ref, line_ref):
    channels = middle_ref.shape[2]
    wide = middle_ref.shape[3]
    rows_in = strip + 2 * EDGE
    rows_out = strip + 2 * (LAYERS - 1)
    lane_ref[...] = jnp.zeros_like(lane_ref)

    def widened(piece, lanes):
        height = piece.shape[0]
        lane_ref[:height, :wide] = piece
        value = lane_ref[:height, :]
        return jnp.concatenate([value, jnp.zeros((height, lanes - 128), F32)], axis=1)

    span = tm_ref.shape[2]
    lanes = -(-span // 128) * 128
    for layer in range(middle_ref.shape[0]):
        base = None
        for a in range(3):
            piece = widened(middle_ref[layer, a].astype(F32), lanes)
            piece = pltpu.roll(piece, a * wide, 1) if a else piece
            base = piece if base is None else base + piece
        for r in range(BAND):
            moved = pltpu.roll(base, r * wide, 1) if r else base
            tm_ref[layer, r * channels : (r + 1) * channels, :] = moved[:, :span].astype(BF16)

    span = t6_ref.shape[1]
    lanes = -(-span // 128) * 128
    base = None
    for a in range(3):
        few_ref[...] = jnp.zeros_like(few_ref)
        few_ref[:2, :wide] = last_ref[a].astype(F32)
        piece = jnp.concatenate([few_ref[...], jnp.zeros((8, lanes - 128), F32)], axis=1)
        piece = pltpu.roll(piece, a * wide, 1) if a else piece
        base = piece if base is None else base + piece
    for r in range(LAST_BAND):
        moved = pltpu.roll(base, r * wide, 1) if r else base
        for o in range(2):
            line_ref[o * LAST_BAND + r, :] = moved[o, :]
    t6_ref[...] = line_ref[:, :span].astype(BF16)

    span = t1_ref.shape[1]
    lanes = -(-span // 128) * 128
    taps = first_ref.shape[2]
    source = lax.broadcasted_iota(jnp.int32, (128, lanes), 0)
    target = lax.broadcasted_iota(jnp.int32, (128, lanes), 1)
    base = None
    for a in range(3):
        lane_ref[...] = jnp.zeros_like(lane_ref)
        lane_ref[:, :taps] = first_ref[a].astype(F32)
        pick = (target == source * rows_in + (EDGE - LAYERS + a)) & (source < taps)
        piece = jnp.dot(
            lane_ref[...].astype(BF16), pick.astype(F32).astype(BF16), preferred_element_type=F32
        )
        base = piece if base is None else base + piece
    for r in range(rows_out):
        moved = pltpu.roll(base, r, 1) if r else base
        t1_ref[r * channels : (r + 1) * channels, :] = moved[:, :span].astype(BF16)


def banded_weights(strip, first_weights, middle_weights, last_weights):
    count, _, channels, wide = middle_weights.shape
    rows_in = strip + 2 * EDGE
    rows_out = strip + 2 * (LAYERS - 1)
    return pl.pallas_call(
        functools.partial(band_kernel, strip),
        out_shape=(
            jax.ShapeDtypeStruct((rows_out * channels, first_weights.shape[2] * rows_in), BF16),
            jax.ShapeDtypeStruct((count, BAND * channels, (BAND + 2) * wide), BF16),
            jax.ShapeDtypeStruct((2 * LAST_BAND, (LAST_BAND + 2) * wide), BF16),
        ),
        in_specs=[VMEM] * 3,
        out_specs=(VMEM,) * 3,
        scratch_shapes=[
            pltpu.VMEM((channels, 128), F32),
            pltpu.VMEM((8, 128), F32),
            pltpu.VMEM((2 * LAST_BAND, -(-(LAST_BAND + 2) * wide // 128) * 128), F32),
        ],
        compiler_params=params(),
        cost_estimate=pl.CostEstimate(flops=10**9, bytes_accessed=3 * 10**6, transcendentals=0),
        name="bands",
    )(first_weights, middle_weights, last_weights)


def strip_kernel(
    where_ref, own_ref, top_ref, bottom_ref, t1_ref, tm_ref, t6_ref, out_ref, x_ref, b0_ref, ba_ref, bb_ref
):
    strip, width = own_ref.shape[1], own_ref.shape[2]
    channels = tm_ref.shape[1] // BAND
    rows_in = strip + 2 * EDGE
    is_first = where_ref[0] == 0
    is_last = where_ref[0] == where_ref[1] - 1
    lane = lax.broadcasted_iota(jnp.int32, (1, width), 1)

    def shifted(value):
        left = jnp.where(lane == 0, 0.0, pltpu.roll(value, 1, 1))
        right = jnp.where(lane == width - 1, 0.0, pltpu.roll(value, width - 1, 1))
        return left, value, right

    for part in range(2):
        x_ref[part, :EDGE, :] = jnp.where(is_first, 0.0, top_ref[part].astype(F32))
        x_ref[part, EDGE : EDGE + strip, :] = own_ref[part]
        x_ref[part, EDGE + strip :, :] = jnp.where(is_last, 0.0, bottom_ref[part].astype(F32))
    for part in range(2):
        for b, value in enumerate(shifted(x_ref[part].astype(BF16).astype(F32))):
            start = (b * 2 + part) * rows_in
            b0_ref[start : start + rows_in, :] = value.astype(BF16)

    def keep(result, row, margin, target):
        low = jnp.where(is_first, margin, 0)
        high = jnp.where(is_last, margin + strip, strip + 2 * margin)
        for j in range(BAND):
            value = jnp.maximum(result[j * channels : (j + 1) * channels, :], 0.0)
            inside = (row + j >= low) & (row + j < high)
            value = jnp.where(inside, value, 0.0)
            for b, moved in enumerate(shifted(value)):
                target[row + j, b * channels : (b + 1) * channels, :] = moved.astype(BF16)

    first_rows = strip + 2 * (LAYERS - 1)
    for start in range(0, first_rows, BAND):
        start = min(start, first_rows - BAND)
        result = jnp.dot(
            t1_ref[start * channels : (start + BAND) * channels, :], b0_ref[...], preferred_element_type=F32
        )
        keep(result, start, LAYERS - 1, ba_ref)

    source, target = ba_ref, bb_ref
    for depth in range(1, LAYERS - 1):
        margin = LAYERS - 1 - depth
        rows = strip + 2 * margin

        def group(number, carry, source=source, target=target, depth=depth, margin=margin, rows=rows):
            row = jnp.minimum(number * BAND, rows - BAND)
            taken = source[pl.ds(row, BAND + 2)]
            result = jnp.dot(
                tm_ref[depth - 1],
                taken.reshape(-1, width),
                preferred_element_type=F32,
            )
            keep(result, row, margin, target)
            return carry

        lax.fori_loop(0, -(-rows // BAND), group, 0)
        source, target = target, source

    for start in range(0, strip, LAST_BAND):
        taken = source[start : start + LAST_BAND + 2]
        result = jnp.dot(t6_ref[...], taken.reshape(-1, width), preferred_element_type=F32)
        for part in range(2):
            own = own_ref[part, start : start + LAST_BAND, :]
            noise = result[part * LAST_BAND : (part + 1) * LAST_BAND, :]
            out_ref[part, start : start + LAST_BAND, :] = own - 2.0 * noise


def prior_reflection(where, prior_state, top, bottom, bands):
    _, strip, width = prior_state.shape
    t1, tm, t6 = bands
    wide = tm.shape[2] // (BAND + 2)
    rows = strip + 2 * (LAYERS - 1)
    return pl.pallas_call(
        strip_kernel,
        out_shape=jax.ShapeDtypeStruct(prior_state.shape, F32),
        in_specs=[SMEM] + [VMEM] * 6,
        out_specs=VMEM,
        scratch_shapes=[
            pltpu.VMEM((2, strip + 2 * EDGE, width), F32),
            pltpu.VMEM((t1.shape[1], width), BF16),
            pltpu.VMEM((rows, wide, width), BF16),
            pltpu.VMEM((rows, wide, width), BF16),
        ],
        compiler_params=params(),
        cost_estimate=pl.CostEstimate(flops=8 * 10**9, bytes_accessed=3 * 10**6, transcendentals=0),
        name="denoise",
    )(where, prior_state, top, bottom, t1, tm, t6)


def gradient_kernel(
    corner_ref,
    flags_ref,
    middle_ref,
    left_ref,
    right_ref,
    measured_ref,
    probe_ref,
    forward_ref,
    backward_ref,
    up_ref,
    down_ref,
    own_ref,
    field_ref,
    total_ref,
    joined_ref,
    stacked_ref,
):
    count = measured_ref.shape[0]
    tall, wide = middle_ref.shape[1], middle_ref.shape[2] + 2 * HALO
    has_left = flags_ref[0] != 0
    has_right = flags_ref[1] != 0
    tile = middle_ref.shape[2]
    for part in range(2):
        field_ref[part, :tall, :HALO] = jnp.where(has_left, left_ref[part].astype(F32), 0.0)
        field_ref[part, :tall, HALO : HALO + tile] = middle_ref[part].astype(F32)
        field_ref[part, :tall, HALO + tile : wide] = jnp.where(has_right, right_ref[part].astype(F32), 0.0)
        field_ref[part, tall:, :] = jnp.zeros((8, wide + 128), F32)
        field_ref[part, :, wide:] = jnp.zeros((tall + 8, 128), F32)
    total_ref[...] = jnp.zeros_like(total_ref)

    lane = lax.broadcasted_iota(jnp.int32, (1, 128), 1)
    sub = lax.broadcasted_iota(jnp.int32, (1, 8, 1), 1)
    tall_load, wide_load = PROBE + 8, PROBE + 128

    def place_of(number):
        top, left = corner_ref[0, number], corner_ref[1, number]
        down, across = lax.rem(top, 8), lax.rem(left, 128)
        rows = pl.ds(pl.multiple_of(top - down, 8), tall_load)
        lanes = pl.ds(pl.multiple_of(left - across, 128), wide_load)
        return rows, lanes, down, across

    def window(part, number):
        rows, lanes, down, across = place_of(number)
        block = field_ref[part, rows, lanes]
        turned = [
            pltpu.roll(block[:, k : k + 128], lax.rem(128 - across, 128), 1) for k in range(0, wide_load, 128)
        ]
        block = jnp.concatenate(
            [jnp.where(lane < 128 - across, low, high) for low, high in zip(turned, turned[1:])], axis=1
        )
        block = pltpu.roll(block.reshape(tall_load // 8, 8, PROBE), lax.rem(8 - down, 8), 1)
        return jnp.where(sub < 8 - down, block[:-1], block[1:]).reshape(PROBE, PROBE)

    def add_window(part, number, terms):
        rows, lanes, down, across = place_of(number)
        block = pltpu.roll(terms.reshape(PROBE // 8, 8, PROBE), down, 1)
        empty = jnp.zeros((1, 8, PROBE), F32)
        block = jnp.where(
            sub >= down, jnp.concatenate([block, empty], axis=0), jnp.concatenate([empty, block], axis=0)
        ).reshape(tall_load, PROBE)
        turned = [pltpu.roll(block[:, k : k + 128], across, 1) for k in range(0, PROBE, 128)]
        empty = jnp.zeros((tall_load, 128), F32)
        block = jnp.concatenate(
            [jnp.where(lane >= across, high, low) for low, high in zip([empty, *turned], [*turned, empty])],
            axis=1,
        )
        total_ref[part, rows, lanes] = total_ref[part, rows, lanes] + block

    for number in range(count):
        real, imag = window(0, number), window(1, number)
        joined_ref[number, :, :PROBE] = (probe_ref[0] * real - probe_ref[1] * imag).astype(BF16)
        joined_ref[number, :, PROBE:] = (probe_ref[0] * imag + probe_ref[1] * real).astype(BF16)
    for number in range(count):
        half = jnp.dot(joined_ref[number], forward_ref[...], preferred_element_type=F32)
        stacked_ref[number, :PROBE, :] = half[:, :PROBE].astype(BF16)
        stacked_ref[number, PROBE:, :] = half[:, PROBE:].astype(BF16)
    for number in range(count):
        wave = jnp.dot(backward_ref[...], stacked_ref[number], preferred_element_type=F32)
        real, imag = wave[:PROBE], wave[PROBE:]
        power = jnp.maximum(real * real + imag * imag, MAGNITUDE_FLOOR * MAGNITUDE_FLOOR)
        retained = 1.0 - measured_ref[number] * lax.rsqrt(power)
        joined_ref[number, :, :PROBE] = (real * retained).astype(BF16)
        joined_ref[number, :, PROBE:] = (imag * retained).astype(BF16)
    for number in range(count):
        back = jnp.dot(joined_ref[number], backward_ref[...], preferred_element_type=F32)
        stacked_ref[number, :PROBE, :] = back[:, :PROBE].astype(BF16)
        stacked_ref[number, PROBE:, :] = back[:, PROBE:].astype(BF16)
    for number in range(count):
        field = jnp.dot(forward_ref[...], stacked_ref[number], preferred_element_type=F32)
        real, imag = field[:PROBE], field[PROBE:]
        add_window(0, number, probe_ref[0] * real + probe_ref[1] * imag)
        add_window(1, number, probe_ref[0] * imag - probe_ref[1] * real)
    for part in range(2):
        up_ref[part] = total_ref[part, :HALO, :wide].astype(BF16)
        own_ref[part] = total_ref[part, HALO : tall - HALO, :wide]
        down_ref[part] = total_ref[part, tall - HALO : tall, :wide].astype(BF16)


def gradient_terms(corners, flags, middle, left, right, measured, probe_field):
    tall = middle.shape[1]
    wide = middle.shape[2] + 2 * HALO
    count = measured.shape[0]
    forward, backward = dft_blocks()
    return pl.pallas_call(
        gradient_kernel,
        out_shape=(
            jax.ShapeDtypeStruct((2, HALO, wide), BF16),
            jax.ShapeDtypeStruct((2, HALO, wide), BF16),
            jax.ShapeDtypeStruct((2, tall - 2 * HALO, wide), F32),
        ),
        in_specs=[SMEM, SMEM] + [VMEM] * 7,
        out_specs=(VMEM,) * 3,
        scratch_shapes=[
            pltpu.VMEM((2, tall + 8, wide + 128), F32),
            pltpu.VMEM((2, tall + 8, wide + 128), F32),
            pltpu.VMEM((count, PROBE, 2 * PROBE), BF16),
            pltpu.VMEM((count, 2 * PROBE, PROBE), BF16),
        ],
        compiler_params=params(),
        cost_estimate=pl.CostEstimate(flops=5 * 10**9, bytes_accessed=4 * 10**6, transcendentals=0),
        name="gradient",
    )(corners, flags, middle, left, right, measured, probe_field, forward, backward)


def parcel_rows(strip, wide, tile, near):
    return 2 * strip * (wide // 128) + 2 * strip + (2 * tile if near else 0)


def gather_kernel(flags_ref, own_ref, above_ref, below_ref, data_ref, prior_ref, mine_ref, tile_ref, *parcels):
    columns = len(parcels) + 1
    strip = prior_ref.shape[1]
    wide = own_ref.shape[2]
    tile = data_ref.shape[2]
    above = flags_ref[0] != 0
    below = flags_ref[1] != 0
    column = flags_ref[2]
    for part in range(2):
        value = own_ref[part]
        value = value + jnp.where(above, above_ref[part].astype(F32), 0.0)
        value = value + jnp.where(below, below_ref[part].astype(F32), 0.0)
        tile_ref[part] = value

    def strip_terms(part, owner):
        start = pl.multiple_of(owner * strip, strip)
        terms = -2.0 * DATA_STEP * tile_ref[part, pl.ds(start, strip), :]
        data = data_ref[part, pl.ds(start, strip), :]
        return [
            terms[:, k * 128 : (k + 1) * 128] + data if k * 128 == HALO else terms[:, k * 128 : (k + 1) * 128]
            for k in range(wide // 128)
        ]

    for distance in range(columns):
        owner = lax.rem(column + distance, columns)
        row = 0
        for part in range(2):
            for k, terms in enumerate(strip_terms(part, owner)):
                if distance == 0:
                    mine_ref[part, :, k * 128 : (k + 1) * 128] = terms
                else:
                    parcels[distance - 1][row : row + strip, :] = terms.astype(BF16)
                row += strip
        if distance == 0:
            continue
        for part in range(2):
            lanes = pl.ds(pl.multiple_of(owner * tile, tile), tile)
            parcels[distance - 1][row : row + strip, :] = prior_ref[part, :, lanes].astype(BF16)
            row += strip
        for far, start in ((1, HALO + tile), (columns - 1, 0)):
            if distance == far:
                for part in range(2):
                    parcels[distance - 1][row : row + tile, :] = tile_ref[
                        part, :, start : start + HALO
                    ].astype(BF16)
                    row += tile


def gather_rows(flags, own, above, below, data_state, prior_reflect, columns):
    strip = prior_reflect.shape[1]
    _, tile, wide = own.shape
    shapes = [jax.ShapeDtypeStruct((2, strip, wide), F32), jax.ShapeDtypeStruct((2, tile, wide), F32)]
    for distance in range(1, columns):
        near = distance in (1, columns - 1)
        shapes.append(jax.ShapeDtypeStruct((parcel_rows(strip, wide, tile, near), 128), BF16))
    return pl.pallas_call(
        gather_kernel,
        out_shape=tuple(shapes),
        in_specs=[SMEM] + [VMEM] * 5,
        out_specs=(VMEM,) * len(shapes),
        compiler_params=params(),
        cost_estimate=pl.CostEstimate(flops=10**8, bytes_accessed=3 * 10**6, transcendentals=0),
        name="parcels",
    )(flags, own, above, below, data_state, prior_reflect)


def update_kernel(flags_ref, mine_ref, tile_ref, data_ref, state_ref, prior_ref, *rest):
    columns = len(rest) - 3 + 1
    parcels = rest[: columns - 1]
    data_out, prior_out, sum_ref = rest[columns - 1 :]
    strip = state_ref.shape[1]
    wide = mine_ref.shape[2]
    tile = data_ref.shape[2]
    column = flags_ref[2]
    blocks = wide // 128
    mixed = 1.0 - DATA_WEIGHT
    sum_ref[...] = jnp.zeros_like(sum_ref)
    for part in range(2):
        lanes = pl.ds(pl.multiple_of(column * tile, tile), wide)
        sum_ref[part, :, lanes] = mine_ref[part]
    for distance in range(1, columns):
        origin = lax.rem(column + columns - distance, columns)
        row = 0
        for part in range(2):
            for k in range(blocks):
                lanes = pl.ds(pl.multiple_of(origin * tile + k * 128, 128), 128)
                terms = parcels[distance - 1][row : row + strip, :].astype(F32)
                sum_ref[part, :, lanes] = sum_ref[part, :, lanes] + terms
                row += strip
    for part in range(2):
        reflect = sum_ref[part, :, HALO : HALO + state_ref.shape[2]]
        prior_out[part] = (
            (1.0 - RELAXATION) * state_ref[part]
            + (RELAXATION * 2.0 * DATA_WEIGHT) * reflect
            + (RELAXATION * (2.0 * mixed - 1.0)) * prior_ref[part]
        )
    near = 2 * strip * blocks + 2 * strip
    from_left = (column > 0, parcels[0])
    from_right = (column < columns - 1, parcels[columns - 2])
    for part in range(2):
        gradient = tile_ref[part, :, HALO : HALO + tile]
        for slot, (present, parcel) in enumerate((from_left, from_right)):
            start = near + part * tile
            if columns == 2:
                start = start + slot * 2 * tile
            terms = parcel[start : start + tile, :].astype(F32)
            gradient = gradient + jnp.where(present, terms, 0.0)
        data = data_ref[part]
        reflect = data - (2.0 * DATA_STEP) * gradient
        data_out[part] = (1.0 - RELAXATION) * data + (RELAXATION * (2.0 * DATA_WEIGHT - 1.0)) * reflect
    weight = RELAXATION * 2.0 * mixed
    for distance in range(columns):
        origin = lax.rem(column + columns - distance, columns)
        rows = pl.ds(pl.multiple_of(origin * strip, strip), strip)
        for part in range(2):
            if distance == 0:
                lanes = pl.ds(pl.multiple_of(column * tile, tile), tile)
                value = prior_ref[part, :, lanes]
            else:
                start = 2 * strip * blocks + part * strip
                value = parcels[distance - 1][start : start + strip, :].astype(F32)
            data_out[part, rows, :] = data_out[part, rows, :] + weight * value


def new_states(flags, mine, gradient, data_state, prior_state, prior_reflect, parcels):
    strip, width = prior_state.shape[1:]
    return pl.pallas_call(
        update_kernel,
        out_shape=(
            jax.ShapeDtypeStruct(data_state.shape, F32),
            jax.ShapeDtypeStruct(prior_state.shape, F32),
        ),
        in_specs=[SMEM] + [VMEM] * (5 + len(parcels)),
        out_specs=(VMEM,) * 2,
        scratch_shapes=[pltpu.VMEM((2, strip, width + 2 * HALO), F32)],
        compiler_params=params(),
        cost_estimate=pl.CostEstimate(flops=10**8, bytes_accessed=3 * 10**6, transcendentals=0),
        name="update",
    )(flags, mine, gradient, data_state, prior_state, prior_reflect, *parcels)


def on_device(
    probe_field,
    offsets,
    amplitudes,
    data_state,
    prior_state,
    first_weights,
    middle_weights,
    last_weights,
):
    tile_rows, tile_cols = data_state.shape[1:]
    strip = prior_state.shape[1]
    grid_rows, grid_cols = tile_rows // STEP, tile_cols // STEP
    columns = lax.axis_size("col")
    row, row_count = lax.axis_index(ROWS), lax.axis_size(ROWS)
    col = lax.axis_index("col")

    small = data_state.astype(BF16)
    from_above = ring(small, ROWS, 1)
    from_below = ring(small, ROWS, -1)
    top = ring(prior_state[:, strip - EDGE :].astype(BF16), STRIPS, 1)
    bottom = ring(prior_state[:, :EDGE].astype(BF16), STRIPS, -1)
    bands = banded_weights(strip, first_weights, middle_weights, last_weights)
    above, below = row > 0, row < row_count - 1
    zero = jnp.zeros_like(small)
    middle = jnp.concatenate(
        [jnp.where(above, from_above, zero), small, jnp.where(below, from_below, zero)], axis=1
    )
    left = ring(middle, "col", 1)
    right = ring(middle, "col", -1)

    base_rows = np.repeat(np.arange(grid_rows) * STEP + JITTER, grid_cols).astype(np.int32)
    base_cols = np.tile(np.arange(grid_cols) * STEP + JITTER, grid_rows).astype(np.int32)
    corners = offsets.reshape(2, -1) + np.stack([base_rows, base_cols])
    flags = jnp.stack([col > 0, col < columns - 1]).astype(jnp.int32)
    up, down, own = gradient_terms(
        corners, flags, middle, left, right, amplitudes.reshape(-1, PROBE, PROBE), probe_field
    )
    below_terms = ring(up, ROWS, -1)
    above_terms = ring(down, ROWS, 1)
    where = jnp.stack([row * columns + col, row_count * columns]).astype(jnp.int32)
    reflect = prior_reflection(where, prior_state, top, bottom, bands)
    flags = jnp.stack([above.astype(jnp.int32), below.astype(jnp.int32), col.astype(jnp.int32)])
    mine, gradient, *parcels = gather_rows(
        flags, own, above_terms, below_terms, data_state, reflect, columns
    )
    parcels = [ring(parcel, "col", number + 1) for number, parcel in enumerate(parcels)]
    return new_states(flags, mine, gradient, data_state, prior_state, reflect, parcels)


def solution(mesh):
    placed = (
        P(),
        P(None, ROWS, "col"),
        P(ROWS, "col", None, None),
        P(None, ROWS, "col"),
        P(None, STRIPS, None),
        P(),
        P(),
        P(),
    )
    return jax.shard_map(
        on_device,
        mesh=mesh,
        in_specs=placed,
        out_specs=(P(None, ROWS, "col"), P(None, STRIPS, None)),
        check_vma=False,
    )
```

time: 149 us -> 58.6 us (0.39)
  the two profiles are of different devices: /device:TPU:10 before, /device:TPU:0 now
where the time goes in v1:
time: 58.6 us; the launch traced here: 58.4 us
  Pallas kernels  24.6 us (42%)
  starting transfers between devices  18.1 us (31%)
  waiting for transfers between devices  12.4 us (21%)
  other arithmetic  1.23 us (2%)
  local copies, waits for them, and re-layouts  1.18 us (2%)
  between operations  0.84 us (1%)
    ppermute x11, starting transfers between devices, ring(): lax.ppermute(value, axes, [(i, (i + shift) % count) for i in range(count)])  18.1 us
    pallas_call x1, Pallas kernels, prior_reflection(): pl.pallas_call(strip_kernel, out_shape=jax.ShapeDtypeStruct(prior_state.s...  17.1 us
    ppermute x11, waiting for transfers between devices, ring(): lax.ppermute(value, axes, [(i, (i + shift) % count) for i in range(count)])  12.4 us
    pallas_call x1, Pallas kernels, gradient_terms(): pl.pallas_call(gradient_kernel, out_shape=(jax.ShapeDtypeStruct((2, HALO,...  4.85 us
    pallas_call x1, Pallas kernels, new_states(): pl.pallas_call(update_kernel, out_shape=(jax.ShapeDtypeStruct(data_state....  1.41 us
  transfers between devices with their start and end apart: 11, of which 4 were waited for; matrix products, arithmetic and copies ran while one was open for 1% of the time, Pallas kernels for 39%

profile of v1, /device:TPU:0, one launch (start us, length us, event | category | flops | bytes accessed | tf_op | source)
XLA Modules:
  0.0 58.4 jit_solution(5556439599741123862)
XLA Ops:
  0.6 0.0 copy-start.1
  0.6 1.0 %convert_element_type.5 = bf16[2,128,128]{2,1,0:T(8,128)(2,1)S(1)} convert(f32[2,128,128]{2,1,0:T(8,128)} %data_ref.3) | non-fusion elementwise | flops 32768 | bytes 196608 | tf_op jit(solution)/shard_map/convert_element_type | solution.py:515
  1.6 6.1 %collective-permute-start.1 = (bf16[2,128,128]{2,1,0:T(8,128)(2,1)S(1)}, bf16[2,128,128]{2,1,0:T(8,128)(2,1)S(1)}, u32[]{:S(2)}, u32[]{:S(2)}) collective-permute-start(bf16[2,128,128]{2,1,0:T(8,128)(2,1)S(1)} %convert_element_type.5), channel_id=1, source_target_pairs={{0,28},{4,0},{8,4},{12,8},{16,12},{20,16},{24,20},{28,24},{1,29},{... | collective-permute-start | bytes 196616 | tf_op jit(solution)/shard_map/ppermute | solution.py:50
  7.7 0.0 collective-permute-start
  7.7 0.0 copy-done.1
  7.7 4.6 %collective-permute-start.7 = (bf16[2,8,512]{2,1,0:T(8,128)(2,1)S(1)}, bf16[2,8,512]{2,1,0:T(8,128)(2,1)S(1)}, u32[]{:S(2)}, u32[]{:S(2)}) collective-permute-start(bf16[2,8,512]{2,1,0:T(8,128)(2,1)S(1)} %get-tuple-element.24), channel_id=1, source_target_pairs={{0,31},{1,0},{2,1},{3,2},{4,3},{5,4},{6,5},{7,6},{8,7},{9,8},{10,9... | collective-permute-start | bytes 49160 | tf_op jit(solution)/shard_map/ppermute | solution.py:50
  12.3 0.0 collective-permute-start.6
  12.3 0.7 %copy-done.9 = s32[2,2,2]{2,1,0:T(2,128)S(1)} copy-done((s32[2,2,2]{2,1,0:T(2,128)S(1)}, s32[2,2,2]{2,1,0:T(2,128)}, u32[]{:S(2)}) %copy-start.9) | copy-done | bytes 56
  13.0 0.0 copy-done.10
  13.0 0.1 reshape.15.corner_ref
  13.1 0.0 copy-done.8
  13.1 0.1 copy.13.first_ref
  13.2 0.1 add_convert_fusion.flags_ref
  13.3 0.1 pad_add_fusion.1.where_ref
  13.4 0.0 collective-permute-done.1
  13.4 1.2 %collective-permute-done = bf16[2,128,128]{2,1,0:T(8,128)(2,1)S(1)} collective-permute-done((bf16[2,128,128]{2,1,0:T(8,128)(2,1)S(1)}, bf16[2,128,128]{2,1,0:T(8,128)(2,1)S(1)}, u32[]{:S(2)}, u32[]{:S(2)}) %collective-permute-start) | collective-permute-done | bytes 65568 | tf_op jit(solution)/shard_map/ppermute | solution.py:50
  14.6 0.0 copy-start.4
  14.6 0.0 copy-start.5
  14.7 0.0 copy-start.2
  14.7 0.0 copy-start.3
  14.7 0.0 copy-start.6
  14.7 0.0 copy-start.7
  14.7 0.1 collective-permute-start.3
  14.8 0.5 collective-permute-start.2
  15.3 0.2 copy-done.4
  15.5 0.0 copy-done.5
  15.5 0.6 bands.1
  16.1 0.1 pad_add_fusion.flags_ref
  16.2 2.9 %collective-permute-done.3.right_ref = bf16[2,384,128]{2,1,0:T(8,128)(2,1)S(1)} collective-permute-done((bf16[2,384,128]{2,1,0:T(8,128)(2,1)S(1)}, bf16[2,384,128]{2,1,0:T(8,128)(2,1)S(1)}, u32[]{:S(2)}, u32[]{:S(2)}) %collective-permute-start.3) | collective-permute-done | bytes 196640 | tf_op jit(solution)/shard_map/ppermute | solution.py:50
  19.1 3.1 %collective-permute-done.2.left_ref = bf16[2,384,128]{2,1,0:T(8,128)(2,1)S(1)} collective-permute-done((bf16[2,384,128]{2,1,0:T(8,128)(2,1)S(1)}, bf16[2,384,128]{2,1,0:T(8,128)(2,1)S(1)}, u32[]{:S(2)}, u32[]{:S(2)}) %collective-permute-start.2) | collective-permute-done | bytes 196640 | tf_op jit(solution)/shard_map/ppermute | solution.py:50
  22.2 0.0 copy-done.2
  22.2 0.0 copy-done.7
  22.2 4.8 %gradient.1 = (bf16[2,128,384]{2,1,0:T(8,128)(2,1)S(1)}, bf16[2,128,384]{2,1,0:T(8,128)(2,1)S(1)}, f32[2,128,384]{2,1,0:T(8,128)S(1)}) custom-call(s32[2,4]{1,0:T(2,128)S(1)} %reshape.15.corner_ref, s32[2]{0:T(128)S(1)} %add_convert_fusion.flags_ref, bf16[2,384,128]{2,1,0:T(8,128)(2,1)S(1)} %pad_maximum_fusion.middle_ref, ...), custom_call_target="tpu_custom_call" | custom-call | flops 5000000000 | bytes 4000000 | tf_op jit(solution)/shard_map/gradient/pallas_call | solution.py:332
  27.1 0.1 collective-permute-start.4
  27.2 4.7 %collective-permute-start.5 = (bf16[2,128,384]{2,1,0:T(8,128)(2,1)S(1)}, bf16[2,128,384]{2,1,0:T(8,128)(2,1)S(1)}, u32[]{:S(2)}, u32[]{:S(2)}) collective-permute-start(bf16[2,128,384]{2,1,0:T(8,128)(2,1)S(1)} %get-tuple-element.15), channel_id=1, source_target_pairs={{0,28},{4,0},{8,4},{12,8},{16,12},{20,16},{24,20},{28,24},{1,29},{... | collective-permute-start | bytes 589832 | tf_op jit(solution)/shard_map/ppermute | solution.py:50
  31.9 0.0 collective-permute-done.7.bottom_ref
  31.9 0.0 collective-permute-done.6.top_ref
  31.9 17.1 %denoise.1.prior_ref = f32[2,32,512]{2,1,0:T(8,128)S(1)} custom-call(s32[2]{0:T(128)S(1)} %pad_add_fusion.1.where_ref, f32[2,32,512]{2,1,0:T(8,128)S(1)} %copy-done.1, bf16[2,8,512]{2,1,0:T(8,128)(2,1)S(1)} %collective-permute-done.6.top_ref, bf16[2,8,512]{2,1,0:T(8,128)(2,1)S(1)} %collective-permute-done.7.bottom_ref, ...), custom_call_target="tpu_custom_call" | custom-call | flops 8000000000 | bytes 3000000 | tf_op jit(solution)/shard_map/denoise/pallas_call | solution.py:211
  49.0 0.0 collective-permute-done.4.above_ref
  49.0 0.0 collective-permute-done.5.below_ref
  49.0 0.7 %parcels.1 = (f32[2,32,384]{2,1,0:T(8,128)S(1)}, f32[2,128,384]{2,1,0:T(8,128)S(1)}, bf16[512,128]{1,0:T(8,128)(2,1)S(1)}, bf16[256,128]{1,0:T(8,128)(2,1)S(1)}, bf16[512,128]{1,0:T(8,128)(2,1)S(1)}) custom-call(s32[3]{0:T(128)S(1)} %pad_add_fusion.flags_ref, f32[2,128,384]{2,1,0:T(8,128)S(1)} %get-tuple-element.13.own_ref, ...), custom_call_target="tpu_custom_call" | custom-call | flops 100000000 | bytes 3000000 | tf_op jit(solution)/shard_map/parcels/pallas_call | solution.py:412
  49.7 0.1 collective-permute-start.8
  49.8 1.7 %collective-permute-start.10 = (bf16[512,128]{1,0:T(8,128)(2,1)S(1)}, bf16[512,128]{1,0:T(8,128)(2,1)S(1)}, u32[]{:S(2)}, u32[]{:S(2)}) collective-permute-start(bf16[512,128]{1,0:T(8,128)(2,1)S(1)} %get-tuple-element.23), channel_id=1, source_target_pairs={{0,3},{1,0},{2,1},{3,2},{4,7},{5,4},{6,5},{7,6},{8,11},{9,8},{10,9... | collective-permute-start | bytes 393224 | tf_op jit(solution)/shard_map/ppermute | solution.py:50
  51.5 0.4 collective-permute-start.9
  51.9 5.1 %collective-permute-done.9.rest_1_ = bf16[256,128]{1,0:T(8,128)(2,1)S(1)} collective-permute-done((bf16[256,128]{1,0:T(8,128)(2,1)S(1)}, bf16[256,128]{1,0:T(8,128)(2,1)S(1)}, u32[]{:S(2)}, u32[]{:S(2)}) %collective-permute-start.9) | collective-permute-done | bytes 65568 | tf_op jit(solution)/shard_map/ppermute | solution.py:50
  57.0 0.0 collective-permute-done.8.rest_0_
  57.0 0.0 collective-permute-done.10.rest_2_
  57.0 1.4 %update.1 = (f32[2,128,128]{2,1,0:T(8,128)}, f32[2,32,512]{2,1,0:T(8,128)}) custom-call(s32[3]{0:T(128)S(1)} %pad_add_fusion.flags_ref, f32[2,32,384]{2,1,0:T(8,128)S(1)} %get-tuple-element.19.mine_ref, f32[2,128,384]{2,1,0:T(8,128)S(1)} %get-tuple-element.20.tile_ref, f32[2,128,128]{2,1,0:T(8,128)S(1)} %copy-done, f32[2,32,512]{2,1,0:T(8,128)S(1)} %copy-done.1, ...), custom_call_target="tpu_custom_call" | custom-call | flops 100000000 | bytes 3000000 | tf_op jit(solution)/shard_map/update/pallas_call | solution.py:483
  (13 shorter events, 0.1 us)
Async XLA Ops:
  0.6 7.0 %copy-start.1 = (f32[2,32,512]{2,1,0:T(8,128)S(1)}, f32[2,32,512]{2,1,0:T(8,128)}, u32[]{:S(2)}) copy-start(f32[2,32,512]{2,1,0:T(8,128)} %state_ref.1) | copy-start | bytes 393220
  1.6 11.8 %collective-permute-start.1 = (bf16[2,128,128]{2,1,0:T(8,128)(2,1)S(1)}, bf16[2,128,128]{2,1,0:T(8,128)(2,1)S(1)}, u32[]{:S(2)}, u32[]{:S(2)}) collective-permute-start(bf16[2,128,128]{2,1,0:T(8,128)(2,1)S(1)} %convert_element_type.5), channel_id=1, source_target_pairs={{0,28},{4,0},{8,4},{12,8},{16,12},{20,16},{24,20},{28,24},{1,29},{... | collective-permute-start | bytes 196616 | tf_op jit(solution)/shard_map/ppermute | solution.py:50
  7.7 7.0 %collective-permute-start = (bf16[2,128,128]{2,1,0:T(8,128)(2,1)S(1)}, bf16[2,128,128]{2,1,0:T(8,128)(2,1)S(1)}, u32[]{:S(2)}, u32[]{:S(2)}) collective-permute-start(bf16[2,128,128]{2,1,0:T(8,128)(2,1)S(1)} %convert_element_type.5), channel_id=1, source_target_pairs={{0,4},{4,8},{8,12},{12,16},{16,20},{20,24},{24,28},{28,0},{1,5},{5... | collective-permute-start | bytes 196616 | tf_op jit(solution)/shard_map/ppermute | solution.py:50
  7.7 24.2 %collective-permute-start.7 = (bf16[2,8,512]{2,1,0:T(8,128)(2,1)S(1)}, bf16[2,8,512]{2,1,0:T(8,128)(2,1)S(1)}, u32[]{:S(2)}, u32[]{:S(2)}) collective-permute-start(bf16[2,8,512]{2,1,0:T(8,128)(2,1)S(1)} %get-tuple-element.24), channel_id=1, source_target_pairs={{0,31},{1,0},{2,1},{3,2},{4,3},{5,4},{6,5},{7,6},{8,7},{9,8},{10,9... | collective-permute-start | bytes 49160 | tf_op jit(solution)/shard_map/ppermute | solution.py:50
  12.3 19.6 %collective-permute-start.6 = (bf16[2,8,512]{2,1,0:T(8,128)(2,1)S(1)}, bf16[2,8,512]{2,1,0:T(8,128)(2,1)S(1)}, u32[]{:S(2)}, u32[]{:S(2)}) collective-permute-start(bf16[2,8,512]{2,1,0:T(8,128)(2,1)S(1)} %get-tuple-element.25), channel_id=1, source_target_pairs={{0,1},{1,2},{2,3},{3,4},{4,5},{5,6},{6,7},{7,8},{8,9},{9,10},{10,1... | collective-permute-start | bytes 49160 | tf_op jit(solution)/shard_map/ppermute | solution.py:50
  12.3 0.7 %copy-start.9 = (s32[2,2,2]{2,1,0:T(2,128)S(1)}, s32[2,2,2]{2,1,0:T(2,128)}, u32[]{:S(2)}) copy-start(s32[2,2,2]{2,1,0:T(2,128)} %param.12) | copy-start | bytes 100
  12.3 0.7 %copy-start.10 = (s32[2,2,2]{2,1,0:T(2,128)S(1)}, s32[2,2,2]{2,1,0:T(2,128)}, u32[]{:S(2)}) copy-start(s32[2,2,2]{2,1,0:T(2,128)} %constant.36) | copy-start | bytes 100
  12.3 0.8 %copy-start.8 = (bf16[3,32,6]{1,2,0:T(8,128)(2,1)S(1)}, bf16[3,32,6]{1,2,0:T(8,128)(2,1)}, u32[]{:S(2)}) copy-start(bf16[3,32,6]{1,2,0:T(8,128)(2,1)} %param.16) | copy-start | bytes 3460
  14.6 0.9 %copy-start.4 = (bf16[4,3,32,96]{3,2,1,0:T(8,128)(2,1)S(1)}, bf16[4,3,32,96]{3,2,1,0:T(8,128)(2,1)}, u32[]{:S(2)}) copy-start(bf16[4,3,32,96]{3,2,1,0:T(8,128)(2,1)} %middle_ref.1) | copy-start | bytes 221188
  14.6 0.9 %copy-start.5 = (bf16[3,2,96]{2,1,0:T(2,128)(2,1)S(1)}, bf16[3,2,96]{2,1,0:T(2,128)(2,1)}, u32[]{:S(2)}) copy-start(bf16[3,2,96]{2,1,0:T(2,128)(2,1)} %last_ref.1) | copy-start | bytes 3460
  14.7 7.5 %copy-start.2 = (f32[2,2,256,256]{3,2,1,0:T(8,128)S(1)}, f32[2,2,256,256]{3,2,1,0:T(8,128)}, u32[]{:S(2)}) copy-start(f32[2,2,256,256]{3,2,1,0:T(8,128)} %param.13) | copy-start | bytes 3145732
  14.7 7.5 %copy-start.3 = (f32[2,256,256]{2,1,0:T(8,128)S(1)}, f32[2,256,256]{2,1,0:T(8,128)}, u32[]{:S(2)}) copy-start(f32[2,256,256]{2,1,0:T(8,128)} %probe_ref.1) | copy-start | bytes 1572868
  14.7 7.5 %copy-start.6 = (bf16[512,512]{1,0:T(8,128)(2,1)S(1)}, bf16[512,512]{1,0:T(8,128)(2,1)}, u32[]{:S(2)}) copy-start(bf16[512,512]{1,0:T(8,128)(2,1)} %constant.33.clone.backward_ref) | copy-start | bytes 1572868
  14.7 7.5 %copy-start.7 = (bf16[512,512]{1,0:T(8,128)(2,1)S(1)}, bf16[512,512]{1,0:T(8,128)(2,1)}, u32[]{:S(2)}) copy-start(bf16[512,512]{1,0:T(8,128)(2,1)} %constant.32.clone.forward_ref) | copy-start | bytes 1572868
  14.7 4.3 %collective-permute-start.3 = (bf16[2,384,128]{2,1,0:T(8,128)(2,1)S(1)}, bf16[2,384,128]{2,1,0:T(8,128)(2,1)S(1)}, u32[]{:S(2)}, u32[]{:S(2)}) collective-permute-start(bf16[2,384,128]{2,1,0:T(8,128)(2,1)S(1)} %pad_maximum_fusion.middle_ref), channel_id=1, source_target_pairs={{0,3},{1,0},{2,1},{3,2},{4,7},{5,4},{6,5},{7,6},{8,11},{9,8},{10,9... | collective-permute-start | bytes 589832 | tf_op jit(solution)/shard_map/ppermute | solution.py:50
  14.8 7.4 %collective-permute-start.2 = (bf16[2,384,128]{2,1,0:T(8,128)(2,1)S(1)}, bf16[2,384,128]{2,1,0:T(8,128)(2,1)S(1)}, u32[]{:S(2)}, u32[]{:S(2)}) collective-permute-start(bf16[2,384,128]{2,1,0:T(8,128)(2,1)S(1)} %pad_maximum_fusion.middle_ref), channel_id=1, source_target_pairs={{0,1},{1,2},{2,3},{3,0},{4,5},{5,6},{6,7},{7,4},{8,9},{9,10},{10,1... | collective-permute-start | bytes 589832 | tf_op jit(solution)/shard_map/ppermute | solution.py:50
  27.1 21.9 %collective-permute-start.4 = (bf16[2,128,384]{2,1,0:T(8,128)(2,1)S(1)}, bf16[2,128,384]{2,1,0:T(8,128)(2,1)S(1)}, u32[]{:S(2)}, u32[]{:S(2)}) collective-permute-start(bf16[2,128,384]{2,1,0:T(8,128)(2,1)S(1)} %get-tuple-element.14), channel_id=1, source_target_pairs={{0,4},{4,8},{8,12},{12,16},{16,20},{20,24},{24,28},{28,0},{1,5},{5... | collective-permute-start | bytes 589832 | tf_op jit(solution)/shard_map/ppermute | solution.py:50
  27.2 21.8 %collective-permute-start.5 = (bf16[2,128,384]{2,1,0:T(8,128)(2,1)S(1)}, bf16[2,128,384]{2,1,0:T(8,128)(2,1)S(1)}, u32[]{:S(2)}, u32[]{:S(2)}) collective-permute-start(bf16[2,128,384]{2,1,0:T(8,128)(2,1)S(1)} %get-tuple-element.15), channel_id=1, source_target_pairs={{0,28},{4,0},{8,4},{12,8},{16,12},{20,16},{24,20},{28,24},{1,29},{... | collective-permute-start | bytes 589832 | tf_op jit(solution)/shard_map/ppermute | solution.py:50
  31.9 17.1 %copy-start = (f32[2,128,128]{2,1,0:T(8,128)S(1)}, f32[2,128,128]{2,1,0:T(8,128)}, u32[]{:S(2)}) copy-start(f32[2,128,128]{2,1,0:T(8,128)} %data_ref.3) | copy-start | bytes 393220
  49.7 7.3 %collective-permute-start.8 = (bf16[512,128]{1,0:T(8,128)(2,1)S(1)}, bf16[512,128]{1,0:T(8,128)(2,1)S(1)}, u32[]{:S(2)}, u32[]{:S(2)}) collective-permute-start(bf16[512,128]{1,0:T(8,128)(2,1)S(1)} %get-tuple-element.21), channel_id=1, source_target_pairs={{0,1},{1,2},{2,3},{3,0},{4,5},{5,6},{6,7},{7,4},{8,9},{9,10},{10,1... | collective-permute-start | bytes 393224 | tf_op jit(solution)/shard_map/ppermute | solution.py:50
  49.8 7.2 %collective-permute-start.10 = (bf16[512,128]{1,0:T(8,128)(2,1)S(1)}, bf16[512,128]{1,0:T(8,128)(2,1)S(1)}, u32[]{:S(2)}, u32[]{:S(2)}) collective-permute-start(bf16[512,128]{1,0:T(8,128)(2,1)S(1)} %get-tuple-element.23), channel_id=1, source_target_pairs={{0,3},{1,0},{2,1},{3,2},{4,7},{5,4},{6,5},{7,6},{8,11},{9,8},{10,9... | collective-permute-start | bytes 393224 | tf_op jit(solution)/shard_map/ppermute | solution.py:50
  51.5 5.5 %collective-permute-start.9 = (bf16[256,128]{1,0:T(8,128)(2,1)S(1)}, bf16[256,128]{1,0:T(8,128)(2,1)S(1)}, u32[]{:S(2)}, u32[]{:S(2)}) collective-permute-start(bf16[256,128]{1,0:T(8,128)(2,1)S(1)} %get-tuple-element.22), channel_id=1, source_target_pairs={{0,2},{1,3},{2,0},{3,1},{4,6},{5,7},{6,4},{7,5},{8,10},{9,11},{10,... | collective-permute-start | bytes 196616 | tf_op jit(solution)/shard_map/ppermute | solution.py:50

commit v2 on v1

--- a/solution.py
+++ b/solution.py
@@ -15,7 +15,7 @@
 LAYERS = 6
 HALO = 128
 EDGE = 8
-BAND = 4
+BAND = 3
 LAST_BAND = 16
 
 MAGNITUDE_FLOOR = 0.5
@@ -48,6 +48,20 @@
 def ring(value, axes, shift):
     count = lax.axis_size(axes)
     return lax.ppermute(value, axes, [(i, (i + shift) % count) for i in range(count)])
+
+
+def swap(value, axes, start, closed):
+    count = lax.axis_size(axes)
+    pairs = []
+    for i in range(count):
+        other = ((i - start) ^ 1) + start
+        pairs.append((i, other % count if closed else other if 0 <= other < count else i))
+    return lax.ppermute(value, axes, pairs)
+
+
+def cross(value, axes, distance):
+    count = lax.axis_size(axes)
+    return lax.ppermute(value, axes, [(i, i ^ distance) for i in range(count)])
 
 
 def band_kernel(strip, first_ref, middle_ref, last_ref, t1_ref, tm_ref, t6_ref, lane_ref, few_ref, line_ref):
@@ -141,12 +155,16 @@
     rows_in = strip + 2 * EDGE
     is_first = where_ref[0] == 0
     is_last = where_ref[0] == where_ref[1] - 1
-    lane = lax.broadcasted_iota(jnp.int32, (1, width), 1)
+    lane = lax.broadcasted_iota(jnp.int32, (1, 128), 1)
 
     def shifted(value):
-        left = jnp.where(lane == 0, 0.0, pltpu.roll(value, 1, 1))
-        right = jnp.where(lane == width - 1, 0.0, pltpu.roll(value, width - 1, 1))
-        return left, value, right
+        tiles = [value[:, k : k + 128] for k in range(0, width, 128)]
+        empty = jnp.zeros_like(tiles[0])
+        down = [pltpu.roll(tile, 1, 1) for tile in tiles]
+        up = [pltpu.roll(tile, 127, 1) for tile in tiles]
+        left = [jnp.where(lane == 0, low, own) for low, own in zip([empty, *down], down)]
+        right = [jnp.where(lane == 127, high, own) for high, own in zip([*up[1:], empty], up)]
+        return jnp.concatenate(left, axis=1), value, jnp.concatenate(right, axis=1)
 
     for part in range(2):
         x_ref[part, :EDGE, :] = jnp.where(is_first, 0.0, top_ref[part].astype(F32))
@@ -157,41 +175,42 @@
             start = (b * 2 + part) * rows_in
             b0_ref[start : start + rows_in, :] = value.astype(BF16)
 
-    def keep(result, row, margin, target):
-        low = jnp.where(is_first, margin, 0)
-        high = jnp.where(is_last, margin + strip, strip + 2 * margin)
+    def keep(result, row, target):
         for j in range(BAND):
             value = jnp.maximum(result[j * channels : (j + 1) * channels, :], 0.0)
-            inside = (row + j >= low) & (row + j < high)
-            value = jnp.where(inside, value, 0.0)
             for b, moved in enumerate(shifted(value)):
                 target[row + j, b * channels : (b + 1) * channels, :] = moved.astype(BF16)
 
-    first_rows = strip + 2 * (LAYERS - 1)
-    for start in range(0, first_rows, BAND):
-        start = min(start, first_rows - BAND)
+    def clear_outside(margin, target):
+        @pl.when(is_first)
+        def _():
+            target[:margin] = jnp.zeros((margin, *target.shape[1:]), BF16)
+
+        @pl.when(is_last)
+        def _():
+            target[margin + strip : strip + 2 * margin] = jnp.zeros((margin, *target.shape[1:]), BF16)
+
+    margin = LAYERS - 1
+    rows = strip + 2 * margin
+    for start in range(0, rows, BAND):
+        start = min(start, rows - BAND)
         result = jnp.dot(
             t1_ref[start * channels : (start + BAND) * channels, :], b0_ref[...], preferred_element_type=F32
         )
-        keep(result, start, LAYERS - 1, ba_ref)
+        keep(result, start, ba_ref)
+    clear_outside(margin, ba_ref)
 
     source, target = ba_ref, bb_ref
     for depth in range(1, LAYERS - 1):
         margin = LAYERS - 1 - depth
         rows = strip + 2 * margin
 
-        def group(number, carry, source=source, target=target, depth=depth, margin=margin, rows=rows):
-            row = jnp.minimum(number * BAND, rows - BAND)
-            taken = source[pl.ds(row, BAND + 2)]
-            result = jnp.dot(
-                tm_ref[depth - 1],
-                taken.reshape(-1, width),
-                preferred_element_type=F32,
-            )
-            keep(result, row, margin, target)
-            return carry
-
-        lax.fori_loop(0, -(-rows // BAND), group, 0)
+        for start in range(0, rows, BAND):
+            start = min(start, rows - BAND)
+            taken = source[start : start + BAND + 2]
+            result = jnp.dot(tm_ref[depth - 1], taken.reshape(-1, width), preferred_element_type=F32)
+            keep(result, start, target)
+        clear_outside(margin, target)
         source, target = target, source
 
     for start in range(0, strip, LAST_BAND):
@@ -229,14 +248,14 @@
     corner_ref,
     flags_ref,
     middle_ref,
-    left_ref,
-    right_ref,
+    near_ref,
+    far_ref,
     measured_ref,
     probe_ref,
     forward_ref,
     backward_ref,
-    up_ref,
-    down_ref,
+    first_ref,
+    second_ref,
     own_ref,
     field_ref,
     total_ref,
@@ -245,13 +264,15 @@
 ):
     count = measured_ref.shape[0]
     tall, wide = middle_ref.shape[1], middle_ref.shape[2] + 2 * HALO
-    has_left = flags_ref[0] != 0
-    has_right = flags_ref[1] != 0
+    odd_row, odd_column = lax.rem(flags_ref[0], 2), lax.rem(flags_ref[2], 2)
+    alone = (flags_ref[2] == 0) | (flags_ref[2] == flags_ref[3] - 1)
     tile = middle_ref.shape[2]
+    near_lanes = pl.ds(pl.multiple_of((1 - odd_column) * (HALO + tile), 128), HALO)
+    far_lanes = pl.ds(pl.multiple_of(odd_column * (HALO + tile), 128), HALO)
     for part in range(2):
-        field_ref[part, :tall, :HALO] = jnp.where(has_left, left_ref[part].astype(F32), 0.0)
+        field_ref[part, :tall, near_lanes] = near_ref[part].astype(F32)
         field_ref[part, :tall, HALO : HALO + tile] = middle_ref[part].astype(F32)
-        field_ref[part, :tall, HALO + tile : wide] = jnp.where(has_right, right_ref[part].astype(F32), 0.0)
+        field_ref[part, :tall, far_lanes] = jnp.where(alone, 0.0, far_ref[part].astype(F32))
         field_ref[part, tall:, :] = jnp.zeros((8, wide + 128), F32)
         field_ref[part, :, wide:] = jnp.zeros((tall + 8, 128), F32)
     total_ref[...] = jnp.zeros_like(total_ref)
@@ -318,13 +339,15 @@
         real, imag = field[:PROBE], field[PROBE:]
         add_window(0, number, probe_ref[0] * real + probe_ref[1] * imag)
         add_window(1, number, probe_ref[0] * imag - probe_ref[1] * real)
+    first_rows = pl.ds(pl.multiple_of((1 - odd_row) * (tall - HALO), 8), HALO)
+    second_rows = pl.ds(pl.multiple_of(odd_row * (tall - HALO), 8), HALO)
     for part in range(2):
-        up_ref[part] = total_ref[part, :HALO, :wide].astype(BF16)
+        first_ref[part] = total_ref[part, first_rows, :wide].astype(BF16)
+        second_ref[part] = total_ref[part, second_rows, :wide].astype(BF16)
         own_ref[part] = total_ref[part, HALO : tall - HALO, :wide]
-        down_ref[part] = total_ref[part, tall - HALO : tall, :wide].astype(BF16)
-
-
-def gradient_terms(corners, flags, middle, left, right, measured, probe_field):
+
+
+def gradient_terms(corners, flags, middle, near, far, measured, probe_field):
     tall = middle.shape[1]
     wide = middle.shape[2] + 2 * HALO
     count = measured.shape[0]
@@ -347,152 +370,172 @@
         compiler_params=params(),
         cost_estimate=pl.CostEstimate(flops=5 * 10**9, bytes_accessed=4 * 10**6, transcendentals=0),
         name="gradient",
-    )(corners, flags, middle, left, right, measured, probe_field, forward, backward)
-
-
-def parcel_rows(strip, wide, tile, near):
-    return 2 * strip * (wide // 128) + 2 * strip + (2 * tile if near else 0)
-
-
-def gather_kernel(flags_ref, own_ref, above_ref, below_ref, data_ref, prior_ref, mine_ref, tile_ref, *parcels):
-    columns = len(parcels) + 1
+    )(corners, flags, middle, near, far, measured, probe_field, forward, backward)
+
+
+DATA_GRADIENT = -2.0 * DATA_STEP * RELAXATION * (2.0 * DATA_WEIGHT - 1.0)
+DATA_PRIOR = 2.0 * RELAXATION * (1.0 - DATA_WEIGHT)
+PRIOR_DATA = 2.0 * RELAXATION * DATA_WEIGHT
+PRIOR_PRIOR = RELAXATION * (1.0 - 2.0 * DATA_WEIGHT)
+
+
+def can_touch(distance):
+    return distance & (distance + 1) == 0
+
+
+def parcel_rows(strip, wide, tile, distance):
+    return 2 * strip * (wide // 128) + 2 * strip + (2 * tile if can_touch(distance) else 0)
+
+
+def strip_terms(tile_ref, data_ref, part, owner, strip):
+    start = pl.multiple_of(owner * strip, strip)
+    terms = (PRIOR_DATA * -2.0 * DATA_STEP) * tile_ref[part, pl.ds(start, strip), :]
+    data = PRIOR_DATA * data_ref[part, pl.ds(start, strip), :]
+    pieces = [terms[:, k : k + 128] for k in range(0, terms.shape[1], 128)]
+    pieces[HALO // 128] = pieces[HALO // 128] + data
+    return pieces
+
+
+def parcel_kernel(flags_ref, own_ref, first_ref, second_ref, data_ref, prior_ref, tile_ref, *parcels):
     strip = prior_ref.shape[1]
-    wide = own_ref.shape[2]
     tile = data_ref.shape[2]
-    above = flags_ref[0] != 0
-    below = flags_ref[1] != 0
+    end = (flags_ref[0] == 0) | (flags_ref[0] == flags_ref[1] - 1)
     column = flags_ref[2]
     for part in range(2):
-        value = own_ref[part]
-        value = value + jnp.where(above, above_ref[part].astype(F32), 0.0)
-        value = value + jnp.where(below, below_ref[part].astype(F32), 0.0)
-        tile_ref[part] = value
-
-    def strip_terms(part, owner):
-        start = pl.multiple_of(owner * strip, strip)
-        terms = -2.0 * DATA_STEP * tile_ref[part, pl.ds(start, strip), :]
-        data = data_ref[part, pl.ds(start, strip), :]
-        return [
-            terms[:, k * 128 : (k + 1) * 128] + data if k * 128 == HALO else terms[:, k * 128 : (k + 1) * 128]
-            for k in range(wide // 128)
-        ]
-
-    for distance in range(columns):
-        owner = lax.rem(column + distance, columns)
+        value = own_ref[part] + first_ref[part].astype(F32)
+        tile_ref[part] = value + jnp.where(end, 0.0, second_ref[part].astype(F32))
+    for distance, parcel in enumerate(parcels, 1):
+        owner = column ^ distance
         row = 0
         for part in range(2):
-            for k, terms in enumerate(strip_terms(part, owner)):
-                if distance == 0:
-                    mine_ref[part, :, k * 128 : (k + 1) * 128] = terms
-                else:
-                    parcels[distance - 1][row : row + strip, :] = terms.astype(BF16)
+            for terms in strip_terms(tile_ref, data_ref, part, owner, strip):
+                parcel[row : row + strip, :] = terms.astype(BF16)
                 row += strip
-        if distance == 0:
-            continue
         for part in range(2):
             lanes = pl.ds(pl.multiple_of(owner * tile, tile), tile)
-            parcels[distance - 1][row : row + strip, :] = prior_ref[part, :, lanes].astype(BF16)
+            parcel[row : row + strip, :] = (DATA_PRIOR * prior_ref[part, :, lanes]).astype(BF16)
             row += strip
-        for far, start in ((1, HALO + tile), (columns - 1, 0)):
-            if distance == far:
-                for part in range(2):
-                    parcels[distance - 1][row : row + tile, :] = tile_ref[
-                        part, :, start : start + HALO
-                    ].astype(BF16)
-                    row += tile
-
-
-def gather_rows(flags, own, above, below, data_state, prior_reflect, columns):
+        if can_touch(distance):
+            lanes = pl.ds(pl.multiple_of(jnp.where(owner > column, HALO + tile, 0), 128), HALO)
+            for part in range(2):
+                parcel[row : row + tile, :] = (DATA_GRADIENT * tile_ref[part, :, lanes]).astype(BF16)
+                row += tile
+
+
+def parcels_of(flags, own, first, second, data_state, prior_reflect, columns):
     strip = prior_reflect.shape[1]
     _, tile, wide = own.shape
-    shapes = [jax.ShapeDtypeStruct((2, strip, wide), F32), jax.ShapeDtypeStruct((2, tile, wide), F32)]
+    shapes = [jax.ShapeDtypeStruct((2, tile, wide), F32)]
     for distance in range(1, columns):
-        near = distance in (1, columns - 1)
-        shapes.append(jax.ShapeDtypeStruct((parcel_rows(strip, wide, tile, near), 128), BF16))
+        shapes.append(jax.ShapeDtypeStruct((parcel_rows(strip, wide, tile, distance), 128), BF16))
     return pl.pallas_call(
-        gather_kernel,
+        parcel_kernel,
         out_shape=tuple(shapes),
         in_specs=[SMEM] + [VMEM] * 5,
         out_specs=(VMEM,) * len(shapes),
         compiler_params=params(),
         cost_estimate=pl.CostEstimate(flops=10**8, bytes_accessed=3 * 10**6, transcendentals=0),
         name="parcels",
-    )(flags, own, above, below, data_state, prior_reflect)
-
-
-def update_kernel(flags_ref, mine_ref, tile_ref, data_ref, state_ref, prior_ref, *rest):
-    columns = len(rest) - 3 + 1
-    parcels = rest[: columns - 1]
-    data_out, prior_out, sum_ref = rest[columns - 1 :]
+    )(flags, own, first, second, data_state, prior_reflect)
+
+
+def base_kernel(flags_ref, tile_ref, data_ref, state_ref, prior_ref, data_out, prior_out):
     strip = state_ref.shape[1]
-    wide = mine_ref.shape[2]
     tile = data_ref.shape[2]
     column = flags_ref[2]
-    blocks = wide // 128
-    mixed = 1.0 - DATA_WEIGHT
-    sum_ref[...] = jnp.zeros_like(sum_ref)
+    own_rows = pl.ds(pl.multiple_of(column * strip, strip), strip)
+    own_lanes = pl.ds(pl.multiple_of(column * tile, tile), tile)
     for part in range(2):
-        lanes = pl.ds(pl.multiple_of(column * tile, tile), wide)
-        sum_ref[part, :, lanes] = mine_ref[part]
-    for distance in range(1, columns):
-        origin = lax.rem(column + columns - distance, columns)
+        data_out[part] = (
+            (1.0 - RELAXATION) + RELAXATION * (2.0 * DATA_WEIGHT - 1.0)
+        ) * data_ref[part] + DATA_GRADIENT * tile_ref[part, :, HALO : HALO + tile]
+        data_out[part, own_rows, :] = data_out[part, own_rows, :] + DATA_PRIOR * prior_ref[part, :, own_lanes]
+        width = state_ref.shape[2]
+        inner = slice(HALO, HALO + width)
+        prior_out[part, :, :HALO] = jnp.zeros((strip, HALO), F32)
+        prior_out[part, :, HALO + width :] = jnp.zeros((strip, HALO), F32)
+        prior_out[part, :, inner] = (1.0 - RELAXATION) * state_ref[part] + PRIOR_PRIOR * prior_ref[part]
+        for k, terms in enumerate(strip_terms(tile_ref, data_ref, part, column, strip)):
+            lanes = pl.ds(pl.multiple_of(column * tile + k * 128, 128), 128)
+            prior_out[part, :, lanes] = prior_out[part, :, lanes] + terms
+
+
+def own_terms(flags, gradient, data_state, prior_state, prior_reflect):
+    _, strip, width = prior_state.shape
+    return pl.pallas_call(
+        base_kernel,
+        out_shape=(
+            jax.ShapeDtypeStruct(data_state.shape, F32),
+            jax.ShapeDtypeStruct((2, strip, width + 2 * HALO), F32),
+        ),
+        in_specs=[SMEM] + [VMEM] * 4,
+        out_specs=(VMEM,) * 2,
+        compiler_params=params(),
+        cost_estimate=pl.CostEstimate(flops=10**9, bytes_accessed=3 * 10**6, transcendentals=0),
+        name="base",
+    )(flags, gradient, data_state, prior_state, prior_reflect)
+
+
+def update_kernel(flags_ref, data_base, prior_base, *rest):
+    *parcels, data_out, prior_out, data_ref, prior_ref, padded_ref, sems = rest
+    strip, width = prior_ref.shape[1], prior_ref.shape[2]
+    tile = data_ref.shape[2]
+    column = flags_ref[2]
+    blocks = 2 * HALO // 128 + tile // 128
+    data_ref[...] = data_base[...]
+    padded_ref[...] = prior_base[...]
+    for distance, parcel in enumerate(parcels, 1):
+        origin = column ^ distance
         row = 0
         for part in range(2):
             for k in range(blocks):
                 lanes = pl.ds(pl.multiple_of(origin * tile + k * 128, 128), 128)
-                terms = parcels[distance - 1][row : row + strip, :].astype(F32)
-                sum_ref[part, :, lanes] = sum_ref[part, :, lanes] + terms
+                terms = parcel[row : row + strip, :].astype(F32)
+                padded_ref[part, :, lanes] = padded_ref[part, :, lanes] + terms
                 row += strip
-    for part in range(2):
-        reflect = sum_ref[part, :, HALO : HALO + state_ref.shape[2]]
-        prior_out[part] = (
-            (1.0 - RELAXATION) * state_ref[part]
-            + (RELAXATION * 2.0 * DATA_WEIGHT) * reflect
-            + (RELAXATION * (2.0 * mixed - 1.0)) * prior_ref[part]
-        )
-    near = 2 * strip * blocks + 2 * strip
-    from_left = (column > 0, parcels[0])
-    from_right = (column < columns - 1, parcels[columns - 2])
-    for part in range(2):
-        gradient = tile_ref[part, :, HALO : HALO + tile]
-        for slot, (present, parcel) in enumerate((from_left, from_right)):
-            start = near + part * tile
-            if columns == 2:
-                start = start + slot * 2 * tile
-            terms = parcel[start : start + tile, :].astype(F32)
-            gradient = gradient + jnp.where(present, terms, 0.0)
-        data = data_ref[part]
-        reflect = data - (2.0 * DATA_STEP) * gradient
-        data_out[part] = (1.0 - RELAXATION) * data + (RELAXATION * (2.0 * DATA_WEIGHT - 1.0)) * reflect
-    weight = RELAXATION * 2.0 * mixed
-    for distance in range(columns):
-        origin = lax.rem(column + columns - distance, columns)
+    prior_ref[...] = padded_ref[:, :, HALO : HALO + width]
+    copy_prior = pltpu.make_async_copy(prior_ref, prior_out, sems.at[0])
+    copy_prior.start()
+    for distance, parcel in enumerate(parcels, 1):
+        origin = column ^ distance
+        row = 2 * strip * blocks
         rows = pl.ds(pl.multiple_of(origin * strip, strip), strip)
         for part in range(2):
-            if distance == 0:
-                lanes = pl.ds(pl.multiple_of(column * tile, tile), tile)
-                value = prior_ref[part, :, lanes]
-            else:
-                start = 2 * strip * blocks + part * strip
-                value = parcels[distance - 1][start : start + strip, :].astype(F32)
-            data_out[part, rows, :] = data_out[part, rows, :] + weight * value
-
-
-def new_states(flags, mine, gradient, data_state, prior_state, prior_reflect, parcels):
-    strip, width = prior_state.shape[1:]
+            data_ref[part, rows, :] = data_ref[part, rows, :] + parcel[row : row + strip, :].astype(F32)
+            row += strip
+        if can_touch(distance):
+            touching = (origin == column + 1) | (origin == column - 1)
+            for part in range(2):
+                terms = parcel[row : row + tile, :].astype(F32)
+                data_ref[part] = data_ref[part] + jnp.where(touching, terms, 0.0)
+                row += tile
+    copy_data = pltpu.make_async_copy(data_ref, data_out, sems.at[1])
+    copy_data.start()
+    copy_prior.wait()
+    copy_data.wait()
+
+
+def new_states(flags, data_base, prior_base, parcels):
+    _, strip, padded = prior_base.shape
+    width = padded - 2 * HALO
     return pl.pallas_call(
         update_kernel,
         out_shape=(
-            jax.ShapeDtypeStruct(data_state.shape, F32),
-            jax.ShapeDtypeStruct(prior_state.shape, F32),
+            jax.ShapeDtypeStruct(data_base.shape, F32),
+            jax.ShapeDtypeStruct((2, strip, width), F32),
         ),
-        in_specs=[SMEM] + [VMEM] * (5 + len(parcels)),
-        out_specs=(VMEM,) * 2,
-        scratch_shapes=[pltpu.VMEM((2, strip, width + 2 * HALO), F32)],
+        in_specs=[SMEM] + [VMEM] * (2 + len(parcels)),
+        out_specs=(pl.BlockSpec(memory_space=pl.ANY),) * 2,
+        scratch_shapes=[
+            pltpu.VMEM(data_base.shape, F32),
+            pltpu.VMEM((2, strip, width), F32),
+            pltpu.VMEM(prior_base.shape, F32),
+            pltpu.SemaphoreType.DMA((2,)),
+        ],
         compiler_params=params(),
         cost_estimate=pl.CostEstimate(flops=10**8, bytes_accessed=3 * 10**6, transcendentals=0),
         name="update",
-    )(flags, mine, gradient, data_state, prior_state, prior_reflect, *parcels)
+    )(flags, data_base, prior_base, *parcels)
 
 
 def on_device(
@@ -508,41 +551,38 @@
     tile_rows, tile_cols = data_state.shape[1:]
     strip = prior_state.shape[1]
     grid_rows, grid_cols = tile_rows // STEP, tile_cols // STEP
-    columns = lax.axis_size("col")
     row, row_count = lax.axis_index(ROWS), lax.axis_size(ROWS)
-    col = lax.axis_index("col")
+    col, columns = lax.axis_index("col"), lax.axis_size("col")
 
     small = data_state.astype(BF16)
-    from_above = ring(small, ROWS, 1)
-    from_below = ring(small, ROWS, -1)
-    top = ring(prior_state[:, strip - EDGE :].astype(BF16), STRIPS, 1)
-    bottom = ring(prior_state[:, :EDGE].astype(BF16), STRIPS, -1)
+    first = swap(small, ROWS, 0, True)
+    second = swap(small, ROWS, 1, True)
     bands = banded_weights(strip, first_weights, middle_weights, last_weights)
-    above, below = row > 0, row < row_count - 1
     zero = jnp.zeros_like(small)
-    middle = jnp.concatenate(
-        [jnp.where(above, from_above, zero), small, jnp.where(below, from_below, zero)], axis=1
-    )
-    left = ring(middle, "col", 1)
-    right = ring(middle, "col", -1)
+    second = jnp.where((row == 0) | (row == row_count - 1), zero, second)
+    odd = row % 2 == 1
+    middle = jnp.concatenate([jnp.where(odd, first, second), small, jnp.where(odd, second, first)], axis=1)
+    near = swap(middle, "col", 0, False)
+    far = swap(middle, "col", 1, False)
+    low, high, _ = lax.optimization_barrier((prior_state[:, strip - EDGE :], prior_state[:, :EDGE], middle))
+    top = ring(low.astype(BF16), STRIPS, 1)
+    bottom = ring(high.astype(BF16), STRIPS, -1)
 
     base_rows = np.repeat(np.arange(grid_rows) * STEP + JITTER, grid_cols).astype(np.int32)
     base_cols = np.tile(np.arange(grid_cols) * STEP + JITTER, grid_rows).astype(np.int32)
     corners = offsets.reshape(2, -1) + np.stack([base_rows, base_cols])
-    flags = jnp.stack([col > 0, col < columns - 1]).astype(jnp.int32)
-    up, down, own = gradient_terms(
-        corners, flags, middle, left, right, amplitudes.reshape(-1, PROBE, PROBE), probe_field
+    flags = jnp.stack([row, jnp.int32(row_count), col, jnp.int32(columns)]).astype(jnp.int32)
+    first, second, own = gradient_terms(
+        corners, flags, middle, near, far, amplitudes.reshape(-1, PROBE, PROBE), probe_field
     )
-    below_terms = ring(up, ROWS, -1)
-    above_terms = ring(down, ROWS, 1)
-    where = jnp.stack([row * columns + col, row_count * columns]).astype(jnp.int32)
+    first = swap(first, ROWS, 0, True)
+    second = swap(second, ROWS, 1, True)
+    where = jnp.stack([row * columns + col, jnp.int32(row_count * columns)]).astype(jnp.int32)
     reflect = prior_reflection(where, prior_state, top, bottom, bands)
-    flags = jnp.stack([above.astype(jnp.int32), below.astype(jnp.int32), col.astype(jnp.int32)])
-    mine, gradient, *parcels = gather_rows(
-        flags, own, above_terms, below_terms, data_state, reflect, columns
-    )
-    parcels = [ring(parcel, "col", number + 1) for number, parcel in enumerate(parcels)]
-    return new_states(flags, mine, gradient, data_state, prior_state, reflect, parcels)
+    gradient, *parcels = parcels_of(flags, own, first, second, data_state, reflect, columns)
+    bases = own_terms(flags, gradient, data_state, prior_state, reflect)
+    parcels = [cross(parcel, "col", distance) for distance, parcel in enumerate(parcels, 1)]
+    return new_states(flags, *bases, parcels)
 
 
 def solution(mesh):

time: 58.6 us -> 44 us (0.75)
  Pallas kernels: 24.6 us -> 15.7 us
  waiting for transfers between devices: 12.4 us -> 9.39 us
  starting transfers between devices: 18.1 us -> 15.8 us
    ppermute x11 -> x2, starting transfers between devices: 18.1 us -> 5.34 us  [ring(): lax.ppermute(value, axes, [(i, (i + shift) % count) for i in range(count)])]
    ppermute x11 -> x2, waiting for transfers between devices: 12.4 us -> 0.01 us  [ring(): lax.ppermute(value, axes, [(i, (i + shift) % count) for i in range(count)])]
    ppermute x0 -> x9, starting transfers between devices: none -> 10.5 us  [the longest x6 8.27 us: swap(): return lax.ppermute(value, axes, pairs)]
    pallas_call x1, Pallas kernels: 17.1 us -> 7.53 us  [prior_reflection(): pl.pallas_call(strip_kernel, out_shape=jax.ShapeDtypeStruct(prior_state.s...]
    ppermute x0 -> x9, waiting for transfers between devices: none -> 9.38 us  [the longest x6 4.95 us: swap(): return lax.ppermute(value, axes, pairs)]
    pallas_call x2 -> x3, Pallas kernels: 2.11 us -> 2.67 us  [the longest x1 1.37 us: new_states(): pl.pallas_call(update_kernel, out_shape=(jax.ShapeDtypeStruct(data_base.s...]
  transfers between devices with their start and end apart: 11 -> 11, of which waited for: 4 -> 3; matrix products, arithmetic and copies ran while one was open for 1% -> 1% of each run, Pallas kernels for 39% -> 31%
where the time goes in v2:
time: 44 us; the launch traced here: 43.8 us
  starting transfers between devices  15.8 us (36%)
  Pallas kernels  15.7 us (36%)
  waiting for transfers between devices  9.39 us (21%)
  other arithmetic  1.12 us (3%)
  local copies, waits for them, and re-layouts  0.96 us (2%)
  between operations  0.84 us (2%)
    ppermute x6, starting transfers between devices, swap(): return lax.ppermute(value, axes, pairs)  8.27 us
    pallas_call x1, Pallas kernels, prior_reflection(): pl.pallas_call(strip_kernel, out_shape=jax.ShapeDtypeStruct(prior_state.s...  7.53 us
    ppermute x2, starting transfers between devices, ring(): lax.ppermute(value, axes, [(i, (i + shift) % count) for i in range(count)])  5.34 us
    ppermute x6, waiting for transfers between devices, swap(): return lax.ppermute(value, axes, pairs)  4.95 us
    pallas_call x1, Pallas kernels, gradient_terms(): pl.pallas_call(gradient_kernel, out_shape=(jax.ShapeDtypeStruct((2, HALO,...  4.91 us
    ppermute x3, waiting for transfers between devices, cross(): return lax.ppermute(value, axes, [(i, i ^ distance) for i in range(count)])  4.43 us
    ppermute x3, starting transfers between devices, cross(): return lax.ppermute(value, axes, [(i, i ^ distance) for i in range(count)])  2.22 us
    pallas_call x1, Pallas kernels, new_states(): pl.pallas_call(update_kernel, out_shape=(jax.ShapeDtypeStruct(data_base.s...  1.37 us
  transfers between devices with their start and end apart: 11, of which 3 were waited for; matrix products, arithmetic and copies ran while one was open for 1% of the time, Pallas kernels for 31%

profile of v2, /device:TPU:0, one launch (start us, length us, event | category | flops | bytes accessed | tf_op | source)
XLA Modules:
  0.0 43.8 jit_solution(14439592626993016110)
XLA Ops:
  0.6 0.0 copy-start.8
  0.6 0.0 copy-start.9
  0.6 0.0 copy-start.10
  0.7 0.9 %convert_element_type.9 = bf16[2,128,128]{2,1,0:T(8,128)(2,1)S(1)} convert(f32[2,128,128]{2,1,0:T(8,128)} %data_ref.3) | non-fusion elementwise | flops 32768 | bytes 196608 | tf_op jit(solution)/shard_map/convert_element_type | solution.py:557
  1.6 0.0 copy-start.4
  1.6 3.1 %collective-permute-start = (bf16[2,128,128]{2,1,0:T(8,128)(2,1)S(1)}, bf16[2,128,128]{2,1,0:T(8,128)(2,1)S(1)}, u32[]{:S(2)}, u32[]{:S(2)}) collective-permute-start(bf16[2,128,128]{2,1,0:T(8,128)(2,1)S(1)} %convert_element_type.9), channel_id=1, source_target_pairs={{0,4},{4,0},{8,12},{12,8},{16,20},{20,16},{24,28},{28,24},{1,5},{5... | collective-permute-start | bytes 196616 | tf_op jit(solution)/shard_map/ppermute | solution.py:59
  4.7 3.4 %collective-permute-start.1 = (bf16[2,128,128]{2,1,0:T(8,128)(2,1)S(1)}, bf16[2,128,128]{2,1,0:T(8,128)(2,1)S(1)}, u32[]{:S(2)}, u32[]{:S(2)}) collective-permute-start(bf16[2,128,128]{2,1,0:T(8,128)(2,1)S(1)} %convert_element_type.9), channel_id=1, source_target_pairs={{0,28},{4,8},{8,4},{12,16},{16,12},{20,24},{24,20},{28,0},{1,29},{... | collective-permute-start | bytes 196616 | tf_op jit(solution)/shard_map/ppermute | solution.py:59
  8.1 0.0 copy-done.8
  8.1 0.1 copy.13.first_ref
  8.2 0.0 copy-done.9
  8.3 0.0 copy-done.10
  8.3 0.1 reshape.13.corner_ref
  8.4 0.1 pad_add_fusion.1.where_ref
  8.4 0.1 pad_add_fusion.flags_ref
  8.5 0.0 copy-done.4
  8.5 0.6 %copy-done.5 = bf16[3,2,96]{2,1,0:T(2,128)(2,1)S(1)} copy-done((bf16[3,2,96]{2,1,0:T(2,128)(2,1)S(1)}, bf16[3,2,96]{2,1,0:T(2,128)(2,1)}, u32[]{:S(2)}) %copy-start.5) | copy-done | bytes 1176
  9.1 0.6 %bands.1 = (bf16[1344,288]{1,0:T(8,128)(2,1)S(1)}, bf16[4,96,480]{2,1,0:T(8,128)(2,1)S(1)}, bf16[32,1728]{1,0:T(8,128)(2,1)S(1)}) custom-call(bf16[3,32,6]{2,1,0:T(8,128)(2,1)S(1)} %copy.13.first_ref, bf16[4,3,32,96]{3,2,1,0:T(8,128)(2,1)S(1)} %copy-done.4, bf16[3,2,96]{2,1,0:T(2,128)(2,1)S(1)} %copy-done.5), custom_call_target="tpu_custom_call" | custom-call | flops 1000000000 | bytes 3000000 | tf_op jit(solution)/shard_map/bands/pallas_call | solution.py:130
  9.7 0.0 copy-start.3
  9.7 0.0 collective-permute-done
  9.7 2.0 %collective-permute-done.1 = bf16[2,128,128]{2,1,0:T(8,128)(2,1)S(1)} collective-permute-done((bf16[2,128,128]{2,1,0:T(8,128)(2,1)S(1)}, bf16[2,128,128]{2,1,0:T(8,128)(2,1)S(1)}, u32[]{:S(2)}, u32[]{:S(2)}) %collective-permute-start.1) | collective-permute-done | bytes 65568 | tf_op jit(solution)/shard_map/ppermute | solution.py:59
  11.8 0.0 copy-start.1
  11.8 0.1 collective-permute-start.2
  11.9 0.7 %collective-permute-start.3 = (bf16[2,384,128]{2,1,0:T(8,128)(2,1)S(1)}, bf16[2,384,128]{2,1,0:T(8,128)(2,1)S(1)}, u32[]{:S(2)}, u32[]{:S(2)}) collective-permute-start(bf16[2,384,128]{2,1,0:T(8,128)(2,1)S(1)} %pad_maximum_fusion.middle_ref), channel_id=1, source_target_pairs={{0,0},{1,2},{2,1},{3,3},{4,4},{5,6},{6,5},{7,7},{8,8},{9,10},{10,9... | collective-permute-start | bytes 589832 | tf_op jit(solution)/shard_map/ppermute | solution.py:59
  12.5 0.1 copy-done.1
  12.7 2.8 %collective-permute-start.6 = (bf16[2,8,512]{2,1,0:T(8,128)(2,1)S(1)}, bf16[2,8,512]{2,1,0:T(8,128)(2,1)S(1)}, u32[]{:S(2)}, u32[]{:S(2)}) collective-permute-start(bf16[2,8,512]{2,1,0:T(8,128)(2,1)S(1)} %get-tuple-element.19), channel_id=1, source_target_pairs={{0,1},{1,2},{2,3},{3,4},{4,5},{5,6},{6,7},{7,8},{8,9},{9,10},{10,1... | collective-permute-start | bytes 49160 | tf_op jit(solution)/shard_map/ppermute | solution.py:50
  15.5 2.5 %collective-permute-start.7 = (bf16[2,8,512]{2,1,0:T(8,128)(2,1)S(1)}, bf16[2,8,512]{2,1,0:T(8,128)(2,1)S(1)}, u32[]{:S(2)}, u32[]{:S(2)}) collective-permute-start(bf16[2,8,512]{2,1,0:T(8,128)(2,1)S(1)} %get-tuple-element.20), channel_id=1, source_target_pairs={{0,31},{1,0},{2,1},{3,2},{4,3},{5,4},{6,5},{7,6},{8,7},{9,8},{10,9... | collective-permute-start | bytes 49160 | tf_op jit(solution)/shard_map/ppermute | solution.py:50
  18.0 0.0 collective-permute-done.2.near_ref
  18.0 0.0 collective-permute-done.3.far_ref
  18.0 0.0 copy-done.2
  18.0 0.0 copy-done.6
  18.0 0.0 copy-done.7
  18.1 4.9 %gradient.1 = (bf16[2,128,384]{2,1,0:T(8,128)(2,1)S(1)}, bf16[2,128,384]{2,1,0:T(8,128)(2,1)S(1)}, f32[2,128,384]{2,1,0:T(8,128)S(1)}) custom-call(s32[2,4]{1,0:T(2,128)S(1)} %reshape.13.corner_ref, s32[4]{0:T(128)S(1)} %pad_add_fusion.flags_ref, bf16[2,384,128]{2,1,0:T(8,128)(2,1)S(1)} %pad_maximum_fusion.middle_ref, ...), custom_call_target="tpu_custom_call" | custom-call | flops 5000000000 | bytes 4000000 | tf_op jit(solution)/shard_map/gradient/pallas_call | solution.py:355
  23.0 0.1 collective-permute-start.4
  23.1 0.9 %collective-permute-start.5 = (bf16[2,128,384]{2,1,0:T(8,128)(2,1)S(1)}, bf16[2,128,384]{2,1,0:T(8,128)(2,1)S(1)}, u32[]{:S(2)}, u32[]{:S(2)}) collective-permute-start(bf16[2,128,384]{2,1,0:T(8,128)(2,1)S(1)} %get-tuple-element.18), channel_id=1, source_target_pairs={{0,28},{4,8},{8,4},{12,16},{16,12},{20,24},{24,20},{28,0},{1,29},{... | collective-permute-start | bytes 589832 | tf_op jit(solution)/shard_map/ppermute | solution.py:59
  24.0 0.0 collective-permute-done.6.top_ref
  24.0 0.0 collective-permute-done.7.bottom_ref
  24.0 7.5 %denoise.1.prior_ref = f32[2,32,512]{2,1,0:T(8,128)S(1)} custom-call(s32[2]{0:T(128)S(1)} %pad_add_fusion.1.where_ref, f32[2,32,512]{2,1,0:T(8,128)S(1)} %copy-done.1, bf16[2,8,512]{2,1,0:T(8,128)(2,1)S(1)} %collective-permute-done.6.top_ref, bf16[2,8,512]{2,1,0:T(8,128)(2,1)S(1)} %collective-permute-done.7.bottom_ref, ...), custom_call_target="tpu_custom_call" | custom-call | flops 8000000000 | bytes 3000000 | tf_op jit(solution)/shard_map/denoise/pallas_call | solution.py:230
  31.5 2.9 %collective-permute-done.4.first_ref = bf16[2,128,384]{2,1,0:T(8,128)(2,1)S(1)} collective-permute-done((bf16[2,128,384]{2,1,0:T(8,128)(2,1)S(1)}, bf16[2,128,384]{2,1,0:T(8,128)(2,1)S(1)}, u32[]{:S(2)}, u32[]{:S(2)}) %collective-permute-start.4) | collective-permute-done | bytes 196640 | tf_op jit(solution)/shard_map/ppermute | solution.py:59
  34.5 0.0 collective-permute-done.5.second_ref
  34.5 0.7 %parcels.1 = (f32[2,128,384]{2,1,0:T(8,128)S(1)}, bf16[512,128]{1,0:T(8,128)(2,1)S(1)}, bf16[256,128]{1,0:T(8,128)(2,1)S(1)}, bf16[512,128]{1,0:T(8,128)(2,1)S(1)}) custom-call(s32[4]{0:T(128)S(1)} %pad_add_fusion.flags_ref, f32[2,128,384]{2,1,0:T(8,128)S(1)} %get-tuple-element.16.own_ref, bf16[2,128,384]{2,1,0:T(8,128)(2,1)S(1)} %collective-permute-done.4.first_ref, ...), custom_call_target="tpu_custom_call" | custom-call | flops 100000000 | bytes 3000000 | tf_op jit(solution)/shard_map/parcels/pallas_call | solution.py:431
  35.2 0.1 collective-permute-start.10
  35.3 1.9 %collective-permute-start.8 = (bf16[512,128]{1,0:T(8,128)(2,1)S(1)}, bf16[512,128]{1,0:T(8,128)(2,1)S(1)}, u32[]{:S(2)}, u32[]{:S(2)}) collective-permute-start(bf16[512,128]{1,0:T(8,128)(2,1)S(1)} %get-tuple-element.27), channel_id=1, source_target_pairs={{0,1},{1,0},{2,3},{3,2},{4,5},{5,4},{6,7},{7,6},{8,9},{9,8},{10,11... | collective-permute-start | bytes 393224 | tf_op jit(solution)/shard_map/ppermute | solution.py:64
  37.2 0.2 collective-permute-start.9
  37.4 0.6 %base.1 = (f32[2,128,128]{2,1,0:T(8,128)S(1)}, f32[2,32,768]{2,1,0:T(8,128)S(1)}) custom-call(s32[4]{0:T(128)S(1)} %pad_add_fusion.flags_ref, f32[2,128,384]{2,1,0:T(8,128)S(1)} %get-tuple-element.24.tile_ref, f32[2,128,128]{2,1,0:T(8,128)S(1)} %copy-done, f32[2,32,512]{2,1,0:T(8,128)S(1)} %copy-done.1, f32[2,32,512]{2,1,0:T(8,128)S(1)} %denoise.1.prior_ref), custom_call_target="tpu_custom_call" | custom-call | flops 1000000000 | bytes 3000000 | tf_op jit(solution)/shard_map/base/pallas_call | solution.py:465
  38.0 4.4 %collective-permute-done.9.rest_1_ = bf16[256,128]{1,0:T(8,128)(2,1)S(1)} collective-permute-done((bf16[256,128]{1,0:T(8,128)(2,1)S(1)}, bf16[256,128]{1,0:T(8,128)(2,1)S(1)}, u32[]{:S(2)}, u32[]{:S(2)}) %collective-permute-start.9) | collective-permute-done | bytes 65568 | tf_op jit(solution)/shard_map/ppermute | solution.py:64
  42.5 0.0 collective-permute-done.10.rest_2_
  42.5 0.0 collective-permute-done.8.rest_0_
  42.5 1.4 %update.1 = (f32[2,128,128]{2,1,0:T(8,128)}, f32[2,32,512]{2,1,0:T(8,128)}) custom-call(s32[4]{0:T(128)S(1)} %pad_add_fusion.flags_ref, f32[2,128,128]{2,1,0:T(8,128)S(1)} %get-tuple-element.25.data_base, f32[2,32,768]{2,1,0:T(8,128)S(1)} %get-tuple-element.26.prior_base, bf16[512,128]{1,0:T(8,128)(2,1)S(1)} %collective-permute-done.8.rest_0_, ...), custom_call_target="tpu_custom_call" | custom-call | flops 100000000 | bytes 3000000 | tf_op jit(solution)/shard_map/update/pallas_call | solution.py:521
  (11 shorter events, 0.1 us)
Async XLA Ops:
  0.6 7.5 %copy-start.8 = (bf16[3,32,6]{1,2,0:T(8,128)(2,1)S(1)}, bf16[3,32,6]{1,2,0:T(8,128)(2,1)}, u32[]{:S(2)}) copy-start(bf16[3,32,6]{1,2,0:T(8,128)(2,1)} %param.16) | copy-start | bytes 3460
  0.6 7.6 %copy-start.9 = (s32[2,2,2]{2,1,0:T(2,128)S(1)}, s32[2,2,2]{2,1,0:T(2,128)}, u32[]{:S(2)}) copy-start(s32[2,2,2]{2,1,0:T(2,128)} %param.12) | copy-start | bytes 100
  0.6 7.6 %copy-start.10 = (s32[2,2,2]{2,1,0:T(2,128)S(1)}, s32[2,2,2]{2,1,0:T(2,128)}, u32[]{:S(2)}) copy-start(s32[2,2,2]{2,1,0:T(2,128)} %constant.51) | copy-start | bytes 100
  1.6 6.9 %copy-start.4 = (bf16[4,3,32,96]{3,2,1,0:T(8,128)(2,1)S(1)}, bf16[4,3,32,96]{3,2,1,0:T(8,128)(2,1)}, u32[]{:S(2)}) copy-start(bf16[4,3,32,96]{3,2,1,0:T(8,128)(2,1)} %middle_ref.1) | copy-start | bytes 221188
  1.6 8.1 %collective-permute-start = (bf16[2,128,128]{2,1,0:T(8,128)(2,1)S(1)}, bf16[2,128,128]{2,1,0:T(8,128)(2,1)S(1)}, u32[]{:S(2)}, u32[]{:S(2)}) collective-permute-start(bf16[2,128,128]{2,1,0:T(8,128)(2,1)S(1)} %convert_element_type.9), channel_id=1, source_target_pairs={{0,4},{4,0},{8,12},{12,8},{16,20},{20,16},{24,28},{28,24},{1,5},{5... | collective-permute-start | bytes 196616 | tf_op jit(solution)/shard_map/ppermute | solution.py:59
  4.7 7.0 %collective-permute-start.1 = (bf16[2,128,128]{2,1,0:T(8,128)(2,1)S(1)}, bf16[2,128,128]{2,1,0:T(8,128)(2,1)S(1)}, u32[]{:S(2)}, u32[]{:S(2)}) collective-permute-start(bf16[2,128,128]{2,1,0:T(8,128)(2,1)S(1)} %convert_element_type.9), channel_id=1, source_target_pairs={{0,28},{4,8},{8,4},{12,16},{16,12},{20,24},{24,20},{28,0},{1,29},{... | collective-permute-start | bytes 196616 | tf_op jit(solution)/shard_map/ppermute | solution.py:59
  8.4 0.7 %copy-start.5 = (bf16[3,2,96]{2,1,0:T(2,128)(2,1)S(1)}, bf16[3,2,96]{2,1,0:T(2,128)(2,1)}, u32[]{:S(2)}) copy-start(bf16[3,2,96]{2,1,0:T(2,128)(2,1)} %last_ref.1) | copy-start | bytes 3460
  9.1 8.9 %copy-start.2 = (f32[2,2,256,256]{3,2,1,0:T(8,128)S(1)}, f32[2,2,256,256]{3,2,1,0:T(8,128)}, u32[]{:S(2)}) copy-start(f32[2,2,256,256]{3,2,1,0:T(8,128)} %param.13) | copy-start | bytes 3145732
  9.1 8.9 %copy-start.6 = (bf16[512,512]{1,0:T(8,128)(2,1)S(1)}, bf16[512,512]{1,0:T(8,128)(2,1)}, u32[]{:S(2)}) copy-start(bf16[512,512]{1,0:T(8,128)(2,1)} %constant.47.clone.forward_ref) | copy-start | bytes 1572868
  9.1 8.9 %copy-start.7 = (bf16[512,512]{1,0:T(8,128)(2,1)S(1)}, bf16[512,512]{1,0:T(8,128)(2,1)}, u32[]{:S(2)}) copy-start(bf16[512,512]{1,0:T(8,128)(2,1)} %constant.48.clone.backward_ref) | copy-start | bytes 1572868
  9.7 8.3 %copy-start.3 = (f32[2,256,256]{2,1,0:T(8,128)S(1)}, f32[2,256,256]{2,1,0:T(8,128)}, u32[]{:S(2)}) copy-start(f32[2,256,256]{2,1,0:T(8,128)} %probe_ref.1) | copy-start | bytes 1572868
  11.8 0.9 %copy-start.1 = (f32[2,32,512]{2,1,0:T(8,128)S(1)}, f32[2,32,512]{2,1,0:T(8,128)}, u32[]{:S(2)}) copy-start(f32[2,32,512]{2,1,0:T(8,128)} %state_ref.1) | copy-start | bytes 393220
  11.8 6.2 %collective-permute-start.2 = (bf16[2,384,128]{2,1,0:T(8,128)(2,1)S(1)}, bf16[2,384,128]{2,1,0:T(8,128)(2,1)S(1)}, u32[]{:S(2)}, u32[]{:S(2)}) collective-permute-start(bf16[2,384,128]{2,1,0:T(8,128)(2,1)S(1)} %pad_maximum_fusion.middle_ref), channel_id=1, source_target_pairs={{0,1},{1,0},{2,3},{3,2},{4,5},{5,4},{6,7},{7,6},{8,9},{9,8},{10,11... | collective-permute-start | bytes 589832 | tf_op jit(solution)/shard_map/ppermute | solution.py:59
  11.9 6.2 %collective-permute-start.3 = (bf16[2,384,128]{2,1,0:T(8,128)(2,1)S(1)}, bf16[2,384,128]{2,1,0:T(8,128)(2,1)S(1)}, u32[]{:S(2)}, u32[]{:S(2)}) collective-permute-start(bf16[2,384,128]{2,1,0:T(8,128)(2,1)S(1)} %pad_maximum_fusion.middle_ref), channel_id=1, source_target_pairs={{0,0},{1,2},{2,1},{3,3},{4,4},{5,6},{6,5},{7,7},{8,8},{9,10},{10,9... | collective-permute-start | bytes 589832 | tf_op jit(solution)/shard_map/ppermute | solution.py:59
  12.7 11.3 %collective-permute-start.6 = (bf16[2,8,512]{2,1,0:T(8,128)(2,1)S(1)}, bf16[2,8,512]{2,1,0:T(8,128)(2,1)S(1)}, u32[]{:S(2)}, u32[]{:S(2)}) collective-permute-start(bf16[2,8,512]{2,1,0:T(8,128)(2,1)S(1)} %get-tuple-element.19), channel_id=1, source_target_pairs={{0,1},{1,2},{2,3},{3,4},{4,5},{5,6},{6,7},{7,8},{8,9},{9,10},{10,1... | collective-permute-start | bytes 49160 | tf_op jit(solution)/shard_map/ppermute | solution.py:50
  15.5 8.5 %collective-permute-start.7 = (bf16[2,8,512]{2,1,0:T(8,128)(2,1)S(1)}, bf16[2,8,512]{2,1,0:T(8,128)(2,1)S(1)}, u32[]{:S(2)}, u32[]{:S(2)}) collective-permute-start(bf16[2,8,512]{2,1,0:T(8,128)(2,1)S(1)} %get-tuple-element.20), channel_id=1, source_target_pairs={{0,31},{1,0},{2,1},{3,2},{4,3},{5,4},{6,5},{7,6},{8,7},{9,8},{10,9... | collective-permute-start | bytes 49160 | tf_op jit(solution)/shard_map/ppermute | solution.py:50
  23.0 11.5 %collective-permute-start.4 = (bf16[2,128,384]{2,1,0:T(8,128)(2,1)S(1)}, bf16[2,128,384]{2,1,0:T(8,128)(2,1)S(1)}, u32[]{:S(2)}, u32[]{:S(2)}) collective-permute-start(bf16[2,128,384]{2,1,0:T(8,128)(2,1)S(1)} %get-tuple-element.17), channel_id=1, source_target_pairs={{0,4},{4,0},{8,12},{12,8},{16,20},{20,16},{24,28},{28,24},{1,5},{5... | collective-permute-start | bytes 589832 | tf_op jit(solution)/shard_map/ppermute | solution.py:59
  23.1 11.4 %collective-permute-start.5 = (bf16[2,128,384]{2,1,0:T(8,128)(2,1)S(1)}, bf16[2,128,384]{2,1,0:T(8,128)(2,1)S(1)}, u32[]{:S(2)}, u32[]{:S(2)}) collective-permute-start(bf16[2,128,384]{2,1,0:T(8,128)(2,1)S(1)} %get-tuple-element.18), channel_id=1, source_target_pairs={{0,28},{4,8},{8,4},{12,16},{16,12},{20,24},{24,20},{28,0},{1,29},{... | collective-permute-start | bytes 589832 | tf_op jit(solution)/shard_map/ppermute | solution.py:59
  24.0 10.5 %copy-start = (f32[2,128,128]{2,1,0:T(8,128)S(1)}, f32[2,128,128]{2,1,0:T(8,128)}, u32[]{:S(2)}) copy-start(f32[2,128,128]{2,1,0:T(8,128)} %data_ref.3) | copy-start | bytes 393220
  35.2 7.3 %collective-permute-start.10 = (bf16[512,128]{1,0:T(8,128)(2,1)S(1)}, bf16[512,128]{1,0:T(8,128)(2,1)S(1)}, u32[]{:S(2)}, u32[]{:S(2)}) collective-permute-start(bf16[512,128]{1,0:T(8,128)(2,1)S(1)} %get-tuple-element.29), channel_id=1, source_target_pairs={{0,3},{1,2},{2,1},{3,0},{4,7},{5,6},{6,5},{7,4},{8,11},{9,10},{10,... | collective-permute-start | bytes 393224 | tf_op jit(solution)/shard_map/ppermute | solution.py:64
  35.3 7.2 %collective-permute-start.8 = (bf16[512,128]{1,0:T(8,128)(2,1)S(1)}, bf16[512,128]{1,0:T(8,128)(2,1)S(1)}, u32[]{:S(2)}, u32[]{:S(2)}) collective-permute-start(bf16[512,128]{1,0:T(8,128)(2,1)S(1)} %get-tuple-element.27), channel_id=1, source_target_pairs={{0,1},{1,0},{2,3},{3,2},{4,5},{5,4},{6,7},{7,6},{8,9},{9,8},{10,11... | collective-permute-start | bytes 393224 | tf_op jit(solution)/shard_map/ppermute | solution.py:64
  37.2 5.3 %collective-permute-start.9 = (bf16[256,128]{1,0:T(8,128)(2,1)S(1)}, bf16[256,128]{1,0:T(8,128)(2,1)S(1)}, u32[]{:S(2)}, u32[]{:S(2)}) collective-permute-start(bf16[256,128]{1,0:T(8,128)(2,1)S(1)} %get-tuple-element.28), channel_id=1, source_target_pairs={{0,2},{1,3},{2,0},{3,1},{4,6},{5,7},{6,4},{7,5},{8,10},{9,11},{10,... | collective-permute-start | bytes 196616 | tf_op jit(solution)/shard_map/ppermute | solution.py:64
